TPU v7x, 8 devices: a whole 2x2x1 slice. The times are simulated.
8 devices in a mesh: rep: 1 (over z), tp: 2 (over y), ep: 4 (over x, core).
Axes of the slice: x: 2, y: 2, z: 1, core: 2. Of those that a mesh axis runs over, the one named last changes fastest.
Arguments:
- hidden: bfloat16 [1024, 1024], P(('rep', 'ep'))
- g_norm: float32 [1024], replicated
- w_q: bfloat16 [1024, 1024], P(None, 'tp')
- w_k: bfloat16 [1024, 512], P(None, 'tp')
- w_v: bfloat16 [1024, 512], P(None, 'tp')
- w_o: bfloat16 [1024, 1024], P('tp')
- k_cache: bfloat16 [1024, 256, 8, 64], P(('rep', 'ep'), None, 'tp')
- v_cache: bfloat16 [1024, 256, 8, 64], P(('rep', 'ep'), None, 'tp')
- lengths: int32 [1024], P(('rep', 'ep'))
- w_sh_gate: bfloat16 [1024, 512], P(None, 'tp')
- w_sh_up: bfloat16 [1024, 512], P(None, 'tp')
- w_sh_down: bfloat16 [512, 1024], P('tp')
- w_gate: bfloat16 [32, 1024, 512], P(('ep', 'tp'))
- w_up: bfloat16 [32, 1024, 512], P(('ep', 'tp'))
- w_down: bfloat16 [32, 512, 1024], P(('ep', 'tp'))
- expert_ids: int32 [1024, 8], P(('rep', 'ep'))
- gate_vals: float32 [1024, 8], P(('rep', 'ep'))
Outputs:
- output: bfloat16 [1024, 1024], P(('rep', 'ep'))
All inputs are finite; a program needn't handle non-finite values.
Results may differ from a plain program's by a relative error of at most 0.00409599.
Values are sent between devices in bfloat16 or wider.
A program may use at most 1 GiB of HBM per device.

v0:
```python
import jax
import jax.numpy as jnp
from jax import lax
from jax.sharding import PartitionSpec as P

RMS_EPS = 1e-6


def rms_norm(hidden, g_norm):
    hid32 = hidden.astype(jnp.float32)
    inv_rms = lax.rsqrt(jnp.mean(hid32 * hid32, axis=-1, keepdims=True) + RMS_EPS)
    return (hid32 * inv_rms * g_norm).astype(jnp.bfloat16)


def local_attention(x_rows, w_q, w_k, w_v, k_cache, v_cache, lengths):
    n_rows, seq_len, kv_local, head_dim = k_cache.shape
    q_per_kv = w_q.shape[1] // (kv_local * head_dim)
    inv_sqrt = head_dim ** -0.5
    q_grp = jnp.dot(x_rows, w_q, preferred_element_type=jnp.float32).astype(jnp.bfloat16).reshape(n_rows, kv_local, q_per_kv, head_dim)
    k_new = jnp.dot(x_rows, w_k, preferred_element_type=jnp.float32).astype(jnp.bfloat16).reshape(n_rows, kv_local, head_dim)
    v_new = jnp.dot(x_rows, w_v, preferred_element_type=jnp.float32).astype(jnp.bfloat16).reshape(n_rows, kv_local, head_dim)
    scores = jnp.einsum('bkgd,bskd->bkgs', q_grp, k_cache, preferred_element_type=jnp.float32) * inv_sqrt
    in_range = jnp.arange(seq_len)[None, None, None, :] < lengths[:, None, None, None]
    scores = jnp.where(in_range, scores, -1e30)
    self_score = jnp.einsum('clhe,cle->clh', q_grp, k_new, preferred_element_type=jnp.float32) * inv_sqrt
    row_peak = jnp.maximum(jnp.max(scores, axis=-1), self_score)
    probs_f32 = jnp.exp(scores - row_peak[..., None])
    self_prob = jnp.exp(self_score - row_peak)
    prob_sum = jnp.sum(probs_f32, axis=-1) + self_prob
    probs_bf = (probs_f32 / prob_sum[..., None]).astype(jnp.bfloat16)
    self_bf = (self_prob / prob_sum).astype(jnp.bfloat16)
    context = jnp.einsum('bkgs,bskd->bkgd', probs_bf, v_cache, preferred_element_type=jnp.float32)
    context = context + self_bf.astype(jnp.float32)[..., None] * v_new.astype(jnp.float32)[:, :, None, :]
    return context.astype(jnp.bfloat16).reshape(n_rows, kv_local * q_per_kv * head_dim)


def dense_partial(x_rows, w_q, w_k, w_v, w_o, k_cache, v_cache, lengths, w_sh_gate, w_sh_up, w_sh_down):
    context = local_attention(x_rows, w_q, w_k, w_v, k_cache, v_cache, lengths)
    attn_part = jnp.dot(context, w_o, preferred_element_type=jnp.float32)
    gate_a = jnp.dot(x_rows, w_sh_gate, preferred_element_type=jnp.float32)
    up_b = jnp.dot(x_rows, w_sh_up, preferred_element_type=jnp.float32)
    act_bf = (jax.nn.silu(gate_a) * up_b).astype(jnp.bfloat16)
    return attn_part + jnp.dot(act_bf, w_sh_down, preferred_element_type=jnp.float32)


def run_experts(recv_rows, row_expert, w_gate, w_up, w_down):
    n_local = w_gate.shape[0]
    sort_order = jnp.argsort(row_expert, stable=True)
    sorted_rows = jnp.take(recv_rows, sort_order, axis=0)
    group_sizes = jnp.sum((row_expert[None, :] == jnp.arange(n_local)[:, None]).astype(jnp.int32), axis=1)
    gate_a = lax.ragged_dot(sorted_rows, w_gate, group_sizes, preferred_element_type=jnp.float32)
    up_b = lax.ragged_dot(sorted_rows, w_up, group_sizes, preferred_element_type=jnp.float32)
    act_bf = (jax.nn.silu(gate_a) * up_b).astype(jnp.bfloat16)
    sorted_out = lax.ragged_dot(act_bf, w_down, group_sizes, preferred_element_type=jnp.float32).astype(jnp.bfloat16)
    return jnp.take(sorted_out, jnp.argsort(sort_order), axis=0)


def solution(mesh):
    tp_size = mesh.shape['tp']
    ep_size = mesh.shape['ep']
    tok_spec = P(('rep', 'ep'), None)
    col_spec = P(None, 'tp')
    row_spec = P('tp', None)
    cache_spec = P(('rep', 'ep'), None, 'tp', None)
    expert_spec = P(('ep', 'tp'), None, None)

    def device_step(hidden, g_norm, w_q, w_k, w_v, w_o, k_cache, v_cache, lengths, w_sh_gate, w_sh_up, w_sh_down, w_gate, w_up, w_down, expert_ids, gate_vals):
        n_rows, top_k = expert_ids.shape
        n_local = w_gate.shape[0]
        capacity = min(n_rows, 2 * n_rows * top_k // (tp_size * ep_size))
        n_slots = ep_size * capacity
        x_rows = rms_norm(hidden, g_norm)
        flat_ids = expert_ids.reshape(-1)
        dest_dev = flat_ids // n_local
        dest_ep = dest_dev // tp_size
        is_mine = (dest_dev % tp_size) == lax.axis_index('tp')
        dest_hits = (dest_ep[:, None] == jnp.arange(ep_size)[None, :]) & is_mine[:, None]
        slot_rank = jnp.cumsum(dest_hits.astype(jnp.int32), axis=0) - 1
        target = jnp.where(is_mine, dest_ep * capacity + jnp.sum(jnp.where(dest_hits, slot_rank, 0), axis=1), n_slots)
        choice_tok = jnp.arange(n_rows * top_k, dtype=jnp.int32) // top_k
        slot_tok = jax.ops.segment_sum(choice_tok, target, num_segments=n_slots)
        slot_exp = jax.ops.segment_sum(flat_ids % n_local + 1, target, num_segments=n_slots)
        send_rows = jnp.take(x_rows, slot_tok, axis=0)
        send_exp = jnp.where(slot_exp > 0, slot_exp - 1, n_local)
        recv_rows = lax.all_to_all(send_rows, 'ep', 0, 0, tiled=True)
        recv_exp = lax.all_to_all(send_exp, 'ep', 0, 0, tiled=True)
        expert_rows = run_experts(recv_rows, recv_exp, w_gate, w_up, w_down)
        returned = lax.all_to_all(expert_rows, 'ep', 0, 0, tiled=True)
        choice_out = jnp.take(returned, jnp.minimum(target, n_slots - 1), axis=0).astype(jnp.float32)
        weighted = jnp.where(is_mine[:, None], choice_out * gate_vals.reshape(-1)[:, None], 0.0)
        routed = jnp.sum(weighted.reshape(n_rows, top_k, -1), axis=1)
        dense = dense_partial(x_rows, w_q, w_k, w_v, w_o, k_cache, v_cache, lengths, w_sh_gate, w_sh_up, w_sh_down)
        total_sum = lax.psum(dense + routed, 'tp')
        return (hidden.astype(jnp.float32) + total_sum).astype(jnp.bfloat16)

    return jax.shard_map(device_step, mesh=mesh, in_specs=(tok_spec, P(None), col_spec, col_spec, col_spec, row_spec, cache_spec, cache_spec, P(('rep', 'ep')), col_spec, col_spec, row_spec, expert_spec, expert_spec, expert_spec, tok_spec, tok_spec), out_specs=tok_spec, check_vma=False)
```

profile of v0, /device:TPU:0, one launch (start us, length us, event | category | flops | bytes accessed | tf_op | source)
XLA Modules:
  0.0 253.3 jit_solution(5889082183861662609)
XLA Ops:
  6.5 0.9 copy.85
  7.9 1.2 reduce-window.6
  9.1 0.2 slice_reduce_fusion
  9.7 11.5 %scatter_custom_fusion.1 = s32[1024]{0:T(1024)S(1)} fusion(s32[2048]{0:T(1024)S(1)} %bitcast.64, s32[2048]{0:T(1024)S(1)} %get-tuple-element.28, s32[]{:T(128)} %constant.123.clone.1), kind=kCustom, calls=%fused_computation.144 | custom fusion | flops 2048 | bytes 4100 | tf_op jit(solution)/shard_map/scatter-add | solution.py:82
  21.2 0.6 add_select_fusion.11
  21.8 4.6 %all-to-all-start.1 = ((s32[4,256,1]{1,2,0:T(1,128)}), s32[4,256,1]{1,2,0:T(1,128)S(1)}, u32[]{:S(2)}, u32[]{:S(2)}) async-start(s32[4,256,1]{1,2,0:T(1,128)} %bitcast.10), calls=%async_computation.1 | async-start | bytes 8192 | tf_op jit(solution)/shard_map/all_to_all | solution.py:86
  26.4 11.5 %scatter_custom_fusion = s32[1024]{0:T(1024)S(1)} fusion(s32[2048]{0:T(1024)S(1)} %bitcast.65, s32[2048]{0:T(1024)S(1)} %add_select_fusion.1, s32[]{:T(128)} %constant.123.clone.1), kind=kCustom, calls=%fused_computation.146 | custom fusion | flops 2048 | bytes 4100 | tf_op jit(solution)/shard_map/scatter-add | solution.py:81
  37.9 1.2 fusion.4
  39.2 1.2 fusion.6
  40.4 5.4 %gather_fusion = bf16[1024,1024]{1,0:T(8,128)(2,1)} fusion(bf16[256,1024]{1,0:T(8,128)(2,1)S(1)} %fusion.6, s32[1024]{0:T(1024)S(1)} %fusion.46), kind=kCustom, calls=%fused_computation.2 | custom fusion | bytes 4198400 | tf_op jit(solution)/shard_map/jit(_take)/gather | solution.py:83
  45.8 0.4 convolution_convert_fusion
  46.4 0.5 copy-done.3
  46.9 0.3 bitcast_convert_fusion
  47.3 0.4 copy.76
  47.9 14.5 %fusion.56 = (f32[256,4,2]{2,1,0:T(4,128)S(1)}, f32[256,4,2,256]{3,2,1,0:T(2,128)}) fusion(bf16[256,4,2,64]{3,2,1,0:T(2,128)(2,1)S(1)} %copy.76, bf16[256,256,4,64]{1,3,2,0:T(8,128)(2,1)} %param.25, pred[256,256]{1,0:T(8,128)(4,1)S(1)} %iota_compare_fusion), kind=kOutput, calls=%fused_computation.152 | convolution fusion | flops 68679680 | bytes 35987456 | tf_op jit(solution)/shard_map/bkgd,bskd->bkgs/dot_general | solution.py:22
  62.4 0.2 copy.77
  62.6 3.2 %broadcast_select_fusion.2 = bf16[4,256,1024]{2,1,0:T(8,128)(2,1)} fusion(bf16[4,256,1024]{2,1,0:T(8,128)(2,1)} %bitcast.54, pred[4,256]{1,0:T(4,128)(4,1)S(1)} %broadcast_in_dim.94), kind=kLoop, calls=%fused_computation.14 | loop fusion | flops 1048576 | bytes 4195328 | tf_op jit(solution)/shard_map/jit(_take)/select_n | solution.py:83
  65.7 0.3 copy.78
  66.0 4.5 %all-to-all-start = ((bf16[4,256,1024]{2,1,0:T(8,128)(2,1)}), bf16[4,256,1024]{2,1,0:T(8,128)(2,1)}, u32[]{:S(2)}, u32[]{:S(2)}) async-start(bf16[4,256,1024]{2,1,0:T(8,128)(2,1)} %broadcast_select_fusion.2), calls=%async_computation | async-start | bytes 4194304 | tf_op jit(solution)/shard_map/all_to_all | solution.py:85
  70.5 7.0 %fusion.3 = f32[256,4,2]{2,1,0:T(4,128)S(1)} fusion(f32[256,4,2,256]{3,2,1,0:T(2,128)} %get-tuple-element.31, f32[256,4,2]{2,1,0:T(4,128)S(1)} %copy.78), kind=kLoop, calls=%fused_computation.27 | loop fusion | flops 1046528 | bytes 2113536 | tf_op jit(solution)/shard_map/reduce_sum | solution.py:29
  77.7 1.0 copy.80
  78.7 1.1 copy.81
  79.8 0.4 convolution_convert_fusion.1
  80.3 4.4 %sort.34 = (s32[1024]{0:T(1024)}, s32[1024]{0:T(1024)S(1)}) sort(s32[1024]{0:T(1024)S(1)} %bitcast.60, s32[1024]{0:T(1024)S(1)} %iota.32), dimensions={0}, to_apply=%region_8.9 | sort | flops 10240 | bytes 16384 | tf_op jit(solution)/shard_map/jit(argsort)/sort | solution.py:48
  84.7 0.6 convert_reduce_fusion
  85.3 1.6 ragged-dot-metadata
  86.9 4.4 %sort.35 = (s32[1024]{0:T(1024)}, s32[1024]{0:T(1024)S(1)}) sort(s32[1024]{0:T(1024)S(1)} %get-tuple-element.8, s32[1024]{0:T(1024)S(1)} %iota.33), dimensions={0}, to_apply=%region_10.12 | sort | flops 10240 | bytes 16384 | tf_op jit(solution)/shard_map/jit(argsort)/sort | solution.py:55
  91.3 4.6 %all-to-all-done = bf16[4,256,1024]{2,1,0:T(8,128)(2,1)} async-done(((bf16[4,256,1024]{2,1,0:T(8,128)(2,1)}), bf16[4,256,1024]{2,1,0:T(8,128)(2,1)}, u32[]{:S(2)}, u32[]{:S(2)}) %all-to-all-start) | async-done | bytes 2097184 | tf_op jit(solution)/shard_map/all_to_all | solution.py:85
  95.9 7.9 %gather_fusion.2 = bf16[1024,1024]{1,0:T(8,128)(2,1)} fusion(bf16[1024,1024]{1,0:T(8,128)(2,1)} %bitcast.13, s32[1024]{0:T(1024)S(1)} %fusion.47), kind=kCustom, calls=%fused_computation.clone | custom fusion | bytes 4198400 | tf_op jit(solution)/shard_map/jit(_take)/gather | solution.py:49
  103.8 3.2 %broadcast_select_fusion.1 = bf16[1024,1024]{1,0:T(8,128)(2,1)} fusion(bf16[1024,1024]{1,0:T(8,128)(2,1)} %gather_fusion.2, pred[1024]{0:T(1024)(128)(4,1)S(1)} %compare_and_fusion.2), kind=kLoop, calls=%fused_computation.13 | loop fusion | flops 1048576 | bytes 4195328 | tf_op jit(solution)/shard_map/jit(_take)/select_n | solution.py:49
  107.0 9.4 %ragged-dot-none.2 = f32[1024,512]{1,0:T(8,128)} custom-call(s32[1]{0:T(128)} %get-tuple-element.10, s32[5]{0:T(128)} %get-tuple-element.11, s32[7]{0:T(128)} %get-tuple-element.12, s32[7]{0:T(128)} %get-tuple-element.13, s32[1]{0:T(128)} %get-tuple-element.10, bf16[1024,1024]{1,0:T(8,128)(2,1)} %broadcast_select_fusion.1, bf16[4,1024,512]{2,1,0:T(8,128)(2,1)} %param.31), custom_call_target="tpu_custom_call" | custom-call | flops 1073741824 | bytes 8388624 | tf_op jit(solution)/shard_map/ragged_dot_general/ragged-dot-none
  116.4 9.4 %ragged-dot-none.1 = f32[1024,512]{1,0:T(8,128)} custom-call(s32[1]{0:T(128)} %get-tuple-element.10, s32[5]{0:T(128)} %get-tuple-element.11, s32[7]{0:T(128)} %get-tuple-element.12, s32[7]{0:T(128)} %get-tuple-element.13, s32[1]{0:T(128)} %get-tuple-element.10, bf16[1024,1024]{1,0:T(8,128)(2,1)} %broadcast_select_fusion.1, bf16[4,1024,512]{2,1,0:T(8,128)(2,1)} %param.32), custom_call_target="tpu_custom_call" | custom-call | flops 1073741824 | bytes 8388624 | tf_op jit(solution)/shard_map/ragged_dot_general/ragged-dot-none
  125.7 3.9 %multiply_convert_fusion = bf16[1024,512]{1,0:T(8,128)(2,1)} fusion(f32[1024,512]{1,0:T(8,128)} %ragged-dot-none.1, f32[1024,512]{1,0:T(8,128)} %ragged-dot-none.2), kind=kLoop, calls=%fused_computation.8 | loop fusion | flops 3145728 | bytes 5242880 | tf_op jit(solution)/shard_map/convert_element_type | solution.py:53
  129.6 9.8 %ragged-dot-none = f32[1024,1024]{1,0:T(8,128)} custom-call(s32[1]{0:T(128)} %get-tuple-element.10, s32[5]{0:T(128)} %get-tuple-element.11, s32[7]{0:T(128)} %get-tuple-element.12, s32[7]{0:T(128)} %get-tuple-element.13, s32[1]{0:T(128)} %get-tuple-element.10, bf16[1024,512]{1,0:T(8,128)(2,1)} %multiply_convert_fusion, bf16[4,512,1024]{2,1,0:T(8,128)(2,1)} %param.33), custom_call_target="tpu_custom_call" | custom-call | flops 1073741824 | bytes 9437200 | tf_op jit(solution)/shard_map/ragged_dot_general/ragged-dot-none
  139.4 3.9 %convert_element_type.77 = bf16[1024,1024]{1,0:T(8,128)(2,1)} convert(f32[1024,1024]{1,0:T(8,128)} %ragged-dot-none) | non-fusion elementwise | flops 1048576 | bytes 6291456 | tf_op jit(solution)/shard_map/convert_element_type | solution.py:54
  143.3 7.9 %gather_fusion.3 = bf16[1024,1024]{1,0:T(8,128)(2,1)} fusion(bf16[1024,1024]{1,0:T(8,128)(2,1)} %convert_element_type.77, s32[1024]{0:T(1024)S(1)} %fusion.48), kind=kCustom, calls=%fused_computation.1.clone | custom fusion | bytes 4198400 | tf_op jit(solution)/shard_map/jit(_take)/gather | solution.py:55
  151.1 3.2 %broadcast_select_fusion = bf16[1024,1024]{1,0:T(8,128)(2,1)} fusion(bf16[1024,1024]{1,0:T(8,128)(2,1)} %gather_fusion.3, pred[1024]{0:T(1024)(128)(4,1)S(1)} %compare_and_fusion.1), kind=kLoop, calls=%fused_computation.12 | loop fusion | flops 1048576 | bytes 4195328 | tf_op jit(solution)/shard_map/jit(_take)/select_n | solution.py:55
  154.4 4.5 %all-to-all-start.2 = ((bf16[4,256,1024]{2,1,0:T(8,128)(2,1)}), bf16[4,256,1024]{2,1,0:T(8,128)(2,1)}, u32[]{:S(2)}, u32[]{:S(2)}) async-start(bf16[4,256,1024]{2,1,0:T(8,128)(2,1)} %bitcast.55), calls=%async_computation.2 | async-start | bytes 4194304 | tf_op jit(solution)/shard_map/all_to_all | solution.py:88
  158.9 15.4 %fusion.1 = bf16[256,4,2,64]{3,2,1,0:T(2,128)(2,1)S(1)} fusion(bf16[256,256,4,64]{1,3,2,0:T(8,128)(2,1)} %param.26, f32[256,4,2,256]{3,2,1,0:T(2,128)} %get-tuple-element.31, f32[256,4,2]{2,1,0:T(4,128)} %copy.80, f32[256,4,2]{2,1,0:T(4,128)S(1)} %copy.78, f32[256,4,64]{2,1,0:T(4,128)S(1)} %copy.82, f32[256,4,2]{2,1,0:T(4,128)} %copy.81), kind=kOutput, calls=%fused_computation.21 | convolution fusion | flops 69074944 | bytes 36200448 | tf_op jit(solution)/shard_map/bkgs,bskd->bkgd/dot_general | solution.py:32
  175.0 0.5 copy.83
  175.5 1.3 fusion.58
  176.8 0.5 fusion.57
  177.3 6.9 %all-to-all-done.2 = bf16[4,256,1024]{2,1,0:T(8,128)(2,1)} async-done(((bf16[4,256,1024]{2,1,0:T(8,128)(2,1)}), bf16[4,256,1024]{2,1,0:T(8,128)(2,1)}, u32[]{:S(2)}, u32[]{:S(2)}) %all-to-all-start.2) | async-done | bytes 2097184 | tf_op jit(solution)/shard_map/all_to_all | solution.py:88
  184.2 12.8 %gather_fusion.1 = bf16[2048,1024]{1,0:T(8,128)(2,1)} fusion(bf16[1024,1024]{1,0:T(8,128)(2,1)} %bitcast.15, s32[2048]{0:T(1024)S(1)} %broadcast_clamp_fusion), kind=kCustom, calls=%fused_computation.3 | custom fusion | bytes 8396800 | tf_op jit(solution)/shard_map/jit(_take)/gather | solution.py:89
  197.1 6.1 %select_reduce_fusion = f32[256,1024]{1,0:T(8,128)} fusion(bf16[2048,1024]{1,0:T(8,128)(2,1)} %gather_fusion.1, f32[256,8]{1,0:T(8,128)S(1)} %copy.91, pred[256,8]{1,0:T(8,128)(4,1)S(1)} %copy.88, pred[256,8]{1,0:T(8,128)(4,1)S(1)} %copy.84), kind=kLoop, calls=%fused_computation.6 | loop fusion | flops 10223616 | bytes 5255168 | tf_op jit(solution)/shard_map/reduce_sum | solution.py:91
  203.2 3.3 %fusion = f32[256,1024]{1,0:T(8,128)} fusion(f32[256,1024]{1,0:T(8,128)} %select_reduce_fusion, f32[256,1024]{1,0:T(8,128)S(1)} %fusion.57, bf16[256,1024]{1,0:T(8,128)(2,1)} %param.30, bf16[256,1024]{1,0:T(8,128)(2,1)S(1)} %fusion.6, bf16[1024,256]{1,0:T(8,128)(2,1)} %param.29, f32[256,256]{1,0:T(8,128)S(1)} %fusion.58), kind=kOutput, calls=%fused_computation.19 | convolution fusion | flops 269352960 | bytes 4980736 | tf_op jit(solution)/shard_map/dot_general | solution.py:43
  206.5 37.8 %all-reduce.2.cloned.1.call-done = f32[256,1024]{1,0:T(8,128)} async-done(((f32[256,1024]{1,0:T(8,128)}), f32[256,1024]{1,0:T(8,128)}) %all-reduce.2.cloned.1.call-update) | async-done | bytes 1048592 | tf_op jit(solution)/shard_map/psum | solution.py:93
  244.3 2.2 fusion.7
  (55 shorter events, 2.4 us)
Async XLA Ops:
  6.5 170.3 %copy-start = (bf16[512,1024]{1,0:T(8,128)(2,1)S(1)}, bf16[512,1024]{1,0:T(8,128)(2,1)}, u32[]{:S(2)}) copy-start(bf16[512,1024]{1,0:T(8,128)(2,1)} %param.24) | copy-start | bytes 3145732
  21.8 44.2 %all-to-all-start.1 = ((s32[4,256,1]{1,2,0:T(1,128)}), s32[4,256,1]{1,2,0:T(1,128)S(1)}, u32[]{:S(2)}, u32[]{:S(2)}) async-start(s32[4,256,1]{1,2,0:T(1,128)} %bitcast.10), calls=%async_computation.1 | async-start | bytes 8192 | tf_op jit(solution)/shard_map/all_to_all | solution.py:86
  40.4 5.4 %copy-start.2 = (bf16[1024,512]{1,0:T(8,128)(2,1)S(1)}, bf16[1024,512]{1,0:T(8,128)(2,1)}, u32[]{:S(2)}) copy-start(bf16[1024,512]{1,0:T(8,128)(2,1)} %param.21) | copy-start | bytes 3145732
  45.8 1.0 copy-start.3
  45.8 1.9 copy-start.7
  66.0 29.9 %all-to-all-start = ((bf16[4,256,1024]{2,1,0:T(8,128)(2,1)}), bf16[4,256,1024]{2,1,0:T(8,128)(2,1)}, u32[]{:S(2)}, u32[]{:S(2)}) async-start(bf16[4,256,1024]{2,1,0:T(8,128)(2,1)} %broadcast_select_fusion.2), calls=%async_computation | async-start | bytes 4194304 | tf_op jit(solution)/shard_map/all_to_all | solution.py:85
  70.5 9.3 %copy-start.4 = (bf16[1024,256]{1,0:T(8,128)(2,1)S(1)}, bf16[1024,256]{1,0:T(8,128)(2,1)}, u32[]{:S(2)}) copy-start(bf16[1024,256]{1,0:T(8,128)(2,1)} %param.23) | copy-start | bytes 1572868
  154.4 29.9 %all-to-all-start.2 = ((bf16[4,256,1024]{2,1,0:T(8,128)(2,1)}), bf16[4,256,1024]{2,1,0:T(8,128)(2,1)}, u32[]{:S(2)}, u32[]{:S(2)}) async-start(bf16[4,256,1024]{2,1,0:T(8,128)(2,1)} %bitcast.55), calls=%async_computation.2 | async-start | bytes 4194304 | tf_op jit(solution)/shard_map/all_to_all | solution.py:88
  158.8 15.6 %copy-start.5 = (s32[256,8]{0,1:T(8,128)S(1)}, s32[256,8]{0,1:T(8,128)}, u32[]{:S(2)}) copy-start(s32[256,8]{0,1:T(8,128)} %param.34) | copy-start | bytes 24580
  158.8 16.0 %copy-start.6 = (f32[256,8]{0,1:T(8,128)S(1)}, f32[256,8]{0,1:T(8,128)}, u32[]{:S(2)}) copy-start(f32[256,8]{0,1:T(8,128)} %param.35) | copy-start | bytes 24580
  158.8 85.5 %all-reduce.2.cloned.1.call-start = ((), (), s32[]{:S(2)}) async-start(), calls=%async_computation.3 | async-start | bytes 2097152 | tf_op jit(solution)/shard_map/psum | solution.py:93
  203.2 41.1 %copy-start.1 = (bf16[256,1024]{1,0:T(8,128)(2,1)S(1)}, bf16[256,1024]{1,0:T(8,128)(2,1)}, u32[]{:S(2)}) copy-start(bf16[256,1024]{1,0:T(8,128)(2,1)} %param.19) | copy-start | bytes 1572868
Sparse Core Ops, SparseCore 0:
  206.6 37.6 all-reduce.1
where the time goes:
time: 252 us; the launch traced here: 253 us
  other arithmetic  69.9 us (28%)
  waiting for transfers between devices  49.3 us (20%)
  local copies, waits for them, and re-layouts  40.6 us (16%)
  matrix products  36.1 us (14%)
  Pallas kernels  30.1 us (12%)
  between operations  13.8 us (5%)
  starting transfers between devices  13.6 us (5%)
    psum x1, waiting for transfers between devices, device_step(): total_sum = lax.psum(dense + routed, 'tp')  37.8 us
    another operation x3, Pallas kernels  28.5 us
    dot_general x1, matrix products, local_attention(): jnp.einsum('bkgs,bskd->bkgd', probs_bf, v_cache, preferred_element_type=j...  15.4 us
    dot_general x1, matrix products, local_attention(): jnp.einsum('bkgd,bskd->bkgs', q_grp, k_cache, preferred_element_type=jnp....  14.5 us
    gather x1, local copies, waits for them, and re-layouts, device_step(): jnp.take(returned, jnp.minimum(target, n_slots - 1), axis=0)  12.8 us
    scatter-add x1, other arithmetic, device_step(): jax.ops.segment_sum(flat_ids % n_local + 1, target, num_segments=n_slots)  11.5 us
    scatter-add x1, other arithmetic, device_step(): slot_tok = jax.ops.segment_sum(choice_tok, target, num_segments=n_slots)  11.5 us
    gather x1, local copies, waits for them, and re-layouts, run_experts(): sorted_rows = jnp.take(recv_rows, sort_order, axis=0)  7.9 us
  transfers between devices with their start and end apart: 4, of which 3 were waited for; matrix products, arithmetic and copies ran while one was open for 30% of the time, Pallas kernels for 1%

commit v1 on v0

v1 whole, which is shorter than its diff:
```python
import functools

import jax
import jax.numpy as jnp
from jax import lax
from jax.experimental import pallas as pl
from jax.experimental.pallas import tpu as pltpu
from jax.sharding import PartitionSpec as P

RMS_EPS = 1e-6
TB = 8
SLOTS = 4
ROWS = 128
LANES = 128
BF = jnp.bfloat16
F32 = jnp.float32


def one_hot_mat(rows, cols, fn):
    r = lax.broadcasted_iota(jnp.int32, (rows, cols), 0)
    c = lax.broadcasted_iota(jnp.int32, (rows, cols), 1)
    return jnp.where(fn(r, c), 1.0, 0.0).astype(BF)


def dotf(a, b):
    return jnp.dot(a, b, preferred_element_type=F32)


def dot_nt(a, b):
    return lax.dot_general(a, b, (((1,), (1,)), ((), ())), preferred_element_type=F32)


def layer_kernel(cfg, hid_hbm, gn_hbm, wq_hbm, wk_hbm, wv_hbm, wo_hbm, k_hbm, v_hbm, len_hbm, wsg_hbm, wsu_hbm, wsd_hbm,
                 wg_hbm, wu_hbm, wd_hbm, ids_hbm, gts_hbm, out_hbm,
                 hall, xall, gn, wq, wk, wv, wo, wsg, wsu, wsd, wg, wu, wd, idg, gtg, gb, kbuf, vbuf, lens,
                 q0, q1, kn, vn, ctx, dense, part, rpf, rph, rx, tx, ry, act, outb,
                 lsem, wsem, ksem, vsem, osem, s_send, s_recv):
    n_rows, kvh, hd, seq, n_local, tp_size, ep_size = cfg
    d_model = hall.shape[2]
    n_chunk = n_rows // ROWS
    n_blk = n_rows // TB
    kd = kvh * hd
    half = ROWS // tp_size
    tp = lax.axis_index('tp')
    ep = lax.axis_index('ep')
    partner = {'ep': ep + 1 - 2 * lax.rem(ep, 2)}
    xnbr = {'ep': lax.rem(ep + ep_size // 2, ep_size)}
    ynbr = {'tp': 1 - tp}

    def local(src, dst, sem):
        return pltpu.make_async_copy(src, dst, sem)

    def remote(i, src, dst, dev):
        return pltpu.make_async_remote_copy(src_ref=src, dst_ref=dst, send_sem=s_send.at[i], recv_sem=s_recv.at[i],
                                            device_id=dev, device_id_type=pl.DeviceIdType.MESH)

    def rows(i):
        return pl.ds(i * ROWS, ROWS)

    hid_cp = [local(hid_hbm, hall.at[0], lsem.at[0])]
    small_cp = [local(ids_hbm, idg.at[0], lsem.at[1]), local(gts_hbm, gtg.at[0], lsem.at[2]),
                local(gn_hbm, gn, lsem.at[3]), local(len_hbm, lens, lsem.at[4])]
    qkv_cp = [local(wq_hbm, wq, lsem.at[5]), local(wk_hbm, wk, lsem.at[6]), local(wv_hbm, wv, lsem.at[7])]
    sh_cp = [local(wsg_hbm, wsg, lsem.at[8]), local(wsu_hbm, wsu, lsem.at[9]), local(wsd_hbm, wsd, lsem.at[10]),
             local(wo_hbm, wo, lsem.at[11])]
    exp_cp = [local(wg_hbm, wg, wsem.at[0]), local(wu_hbm, wu, wsem.at[1]), local(wd_hbm, wd, wsem.at[2])]

    def kv_cp(b, slot):
        at = pl.ds(b * TB, TB)
        return (local(k_hbm.at[at], kbuf.at[slot], ksem.at[slot]), local(v_hbm.at[at], vbuf.at[slot], vsem.at[slot]))

    for c in hid_cp + small_cp + qkv_cp:
        c.start()
    for b in range(SLOTS):
        for c in kv_cp(b, b):
            c.start()
    for c in exp_cp + sh_cp:
        c.start()

    barrier = pltpu.get_barrier_semaphore()
    for dev in (partner, xnbr, ynbr):
        pl.semaphore_signal(barrier, inc=1, device_id=dev, device_id_type=pl.DeviceIdType.MESH)
    pl.semaphore_wait(barrier, 3)

    x_hid = [remote(i, hall.at[0, rows(i)], hall.at[2, rows(i)], xnbr) for i in range(n_chunk)]
    p_hid = [remote(2 + i, hall.at[0, rows(i)], hall.at[1, rows(i)], partner) for i in range(n_chunk)]
    f_hid = [remote(4 + i, hall.at[2, rows(i)], hall.at[3, rows(i)], partner) for i in range(n_chunk)]
    x_idg = [remote(6, idg.at[0], idg.at[2], xnbr), remote(7, gtg.at[0], gtg.at[2], xnbr)]
    p_idg = [remote(8, idg.at[0], idg.at[1], partner), remote(9, gtg.at[0], gtg.at[1], partner)]
    f_idg = [remote(10, idg.at[2], idg.at[3], partner), remote(11, gtg.at[2], gtg.at[3], partner)]
    c_far = [remote(12 + i, part.at[3, rows(i)], rpf.at[rows(i)], partner) for i in range(n_chunk)]
    x_ret = [remote(14 + i, part.at[2, rows(i)], rx.at[rows(i)], xnbr) for i in range(n_chunk)]
    c_near = [remote(16 + i, part.at[1, rows(i)], rph.at[rows(i)], partner) for i in range(n_chunk)]

    def mine(i):
        return pl.ds(pl.multiple_of(i * ROWS + tp * half, half), half)

    def theirs(i):
        return pl.ds(pl.multiple_of(i * ROWS + (1 - tp) * half, half), half)

    y_sum = [remote(18 + i, tx.at[i], ry.at[i], ynbr) for i in range(n_chunk)]
    y_out = [remote(20 + i, outb.at[mine(i)], outb.at[mine(i)], ynbr) for i in range(n_chunk)]

    for c in small_cp:
        c.wait()
    for c in x_idg + p_idg:
        c.start()
    for c in hid_cp:
        c.wait()
    for c in x_hid + p_hid:
        c.start()

    def normalize(grp, r0, n):
        def body(j, carry):
            at = pl.ds(pl.multiple_of(r0 + j * 32, 32), 32)
            h32 = hall[grp, at, :].astype(F32)
            inv = lax.rsqrt(jnp.mean(h32 * h32, axis=-1, keepdims=True) + RMS_EPS)
            xall[grp, at, :] = (h32 * inv * gn[...]).astype(BF)
            return carry
        lax.fori_loop(0, n // 32, body, 0)

    first_exp = (ep * tp_size + tp) * n_local

    def gate_table(grp):
        ids = idg[grp]
        vals = gtg[grp]
        picked = [jnp.sum(jnp.where(ids == first_exp + e, vals, 0.0), axis=0, keepdims=True) for e in range(n_local)]
        table = jnp.concatenate(picked + [jnp.zeros((LANES - n_local, n_rows), F32)], axis=0)
        cols = jnp.transpose(table)
        for e in range(n_local):
            gb[grp, e] = jnp.broadcast_to(cols[:, e:e + 1], (n_rows, LANES))

    normalize(0, 0, n_rows)
    for c in qkv_cp:
        c.wait()

    nq = wq.shape[1]
    q_bf = [dotf(xall[0], wq[:, j * 256:(j + 1) * 256]).astype(BF) for j in range(nq // 256)]
    for g, ref in enumerate((q0, q1)):
        acc = None
        for j in range(nq // 256):
            def sel(r, c, j=j, g=g):
                rr = r + j * 256
                return ((rr // (2 * hd)) == (c // hd)) & ((rr % (2 * hd)) == g * hd + c % hd)
            term = dotf(q_bf[j], one_hot_mat(256, kd, sel))
            acc = term if acc is None else acc + term
        ref[...] = acc
    kn[...] = dotf(xall[0], wk[...]).astype(BF).astype(F32)
    vn[...] = dotf(xall[0], wv[...]).astype(BF).astype(F32)

    R = TB * 2 * kvh
    per_tok = 2 * kvh
    expand_q = one_hot_mat(R, 2 * TB, lambda r, c: c == ((r % per_tok) // kvh) * TB + r // per_tok)
    expand_n = one_hot_mat(R, TB, lambda r, c: c == r // per_tok)
    gather_o = one_hot_mat(2 * TB, R, lambda r, c: (c // per_tok == r % TB) & ((c % per_tok) // kvh == r // TB))
    rr = lax.broadcasted_iota(jnp.int32, (R, kd), 0)
    cc = lax.broadcasted_iota(jnp.int32, (R, kd), 1)
    own = (rr % kvh) == (cc // hd)
    pos = lax.broadcasted_iota(jnp.int32, (per_tok, seq), 1)
    scale = hd ** -0.5

    def attn_block(b, carry):
        slot = lax.rem(b, SLOTS)
        tok = pl.ds(pl.multiple_of(b * TB, TB), TB)
        kc, vc = kv_cp(b, slot)
        qq = jnp.concatenate([q0[tok, :], q1[tok, :]], axis=0).astype(BF)
        q_blk = jnp.where(own, dotf(expand_q, qq), 0.0)
        k_self = dotf(expand_n, kn[tok, :].astype(BF))
        v_self = dotf(expand_n, vn[tok, :].astype(BF))
        self_score = jnp.sum(q_blk * k_self, axis=-1, keepdims=True) * scale
        kc.wait()
        parts = []
        for t in range(TB):
            s_t = dotf(q_blk[t * per_tok:(t + 1) * per_tok].astype(BF), kbuf[slot, t])
            parts.append(jnp.where(pos < lens[b * TB + t], s_t * scale, -1e30))
        scores = jnp.concatenate(parts, axis=0)
        peak = jnp.maximum(jnp.max(scores, axis=-1, keepdims=True), self_score)
        prob = jnp.exp(scores - peak)
        self_prob = jnp.exp(self_score - peak)
        inv = 1.0 / (jnp.sum(prob, axis=-1, keepdims=True) + self_prob)
        prob = prob * inv
        self_bf = (self_prob * inv).astype(BF).astype(F32)
        vc.wait()
        outs = [dot_nt(prob[t * per_tok:(t + 1) * per_tok].astype(BF), vbuf[slot, t]) for t in range(TB)]
        o = jnp.concatenate(outs, axis=0) + self_bf * v_self
        o = jnp.where(own, o, 0.0).astype(BF)
        o2 = dotf(gather_o, o)
        ctx[tok, 0:kd] = o2[0:TB]
        ctx[tok, kd:2 * kd] = o2[TB:2 * TB]

        @pl.when(b + SLOTS < n_blk)
        def _():
            for c in kv_cp(b + SLOTS, slot):
                c.start()
        return carry

    def attend(lo, hi):
        lax.fori_loop(lo, hi, attn_block, 0)

    ff = wg.shape[2]

    def unit(grp, r0):
        at = pl.ds(r0, ROWS)

        def body(e, carry):
            xr = xall[grp, at, :]
            for j in range(ff // 256):
                cs = slice(j * 256, (j + 1) * 256)
                g_a = dotf(xr, wg[e, :, cs])
                u_b = dotf(xr, wu[e, :, cs])
                act[:, cs] = (g_a * jax.nn.sigmoid(g_a) * u_b).astype(BF)
            gate = gb[grp, e, at, :]
            hit = gate > 0.0
            first = e == 0
            for j in range(d_model // 256):
                y = dotf(act[...], wd[e, :, j * 256:(j + 1) * 256]).astype(BF).astype(F32)
                for m in range(256 // LANES):
                    ls = slice(j * 256 + m * LANES, j * 256 + (m + 1) * LANES)
                    add = jnp.where(hit, gate * y[:, m * LANES:(m + 1) * LANES], 0.0)
                    part[grp, at, ls] = jnp.where(first, add, part[grp, at, ls] + add)
            return carry

        lax.fori_loop(0, n_local, body, 0)

    splits = [n_blk * s // 32 for s in (0, 8, 13, 32)]
    attend(splits[0], splits[1])
    for c in x_idg + p_idg:
        c.wait_recv()
    for c in f_idg:
        c.start()
    x_hid[0].wait_recv()
    f_hid[0].start()
    gate_table(0)
    gate_table(1)
    gate_table(2)
    normalize(2, 0, ROWS)
    attend(splits[1], splits[2])
    for i in range(1, n_chunk):
        x_hid[i].wait_recv()
        f_hid[i].start()
        normalize(2, i * ROWS, ROWS)
    for c in f_idg:
        c.wait_recv()
    gate_table(3)
    for c in exp_cp:
        c.wait()
    for i in range(n_chunk):
        f_hid[i].wait_recv()
        normalize(3, i * ROWS, ROWS)
        unit(3, i * ROWS)
        c_far[i].start()
        unit(2, i * ROWS)
        c_far[i].wait_recv()
        at = rows(i)
        part[2, at, :] = part[2, at, :] + rpf[at, :]
        x_ret[i].start()
    for i in range(n_chunk):
        p_hid[i].wait_recv()
        normalize(1, i * ROWS, ROWS)
        unit(1, i * ROWS)
        c_near[i].start()
    for i in range(n_chunk):
        unit(0, i * ROWS)
    attend(splits[2], splits[3])

    for c in sh_cp:
        c.wait()
    swap = one_hot_mat(2 * kd, 2 * kd, lambda r, c: ((r // kd) == ((c // hd) % 2)) & ((r % kd) // hd == c // (2 * hd)) & (r % hd == c % hd))
    ctx_bf = dotf(ctx[...].astype(BF), swap).astype(BF)
    sg = dotf(xall[0], wsg[...])
    su = dotf(xall[0], wsu[...])
    sa = (sg * jax.nn.sigmoid(sg) * su).astype(BF)
    for j in range(d_model // 256):
        cs = slice(j * 256, (j + 1) * 256)
        dense[:, cs] = dotf(ctx_bf, wo[:, cs]) + dotf(sa, wsd[:, cs]) + part[0, :, cs]

    for i in range(n_chunk):
        c_near[i].wait_recv()
        x_ret[i].wait_recv()
        at = theirs(i)
        tx[i] = dense[at, :] + rph[at, :] + rx[at, :]
        y_sum[i].start()
    out_cp = []
    for i in range(n_chunk):
        y_sum[i].wait_recv()
        at = mine(i)
        outb[at, :] = (hall[0, at, :].astype(F32) + (dense[at, :] + rph[at, :] + rx[at, :] + ry[i])).astype(BF)
        y_out[i].start()
    for i in range(n_chunk):
        y_out[i].wait_recv()
        c = local(outb.at[rows(i)], out_hbm.at[rows(i)], osem.at[i])
        c.start()
        out_cp.append(c)
    for c in x_hid + p_hid + f_hid + x_idg + p_idg + f_idg + c_far + x_ret + c_near + y_sum + y_out:
        c.wait_send()
    for c in out_cp:
        c.wait()


def solution(mesh):
    tp_size = mesh.shape['tp']
    ep_size = mesh.shape['ep']
    tok_spec = P(('rep', 'ep'), None)
    col_spec = P(None, 'tp')
    row_spec = P('tp', None)
    cache_spec = P(('rep', 'ep'), None, 'tp', None)
    expert_spec = P(('ep', 'tp'), None, None)

    def device_step(hidden, g_norm, w_q, w_k, w_v, w_o, k_cache, v_cache, lengths, w_sh_gate, w_sh_up, w_sh_down, w_gate, w_up, w_down, expert_ids, gate_vals):
        n_rows, d = hidden.shape
        _, seq, kvh, hd = k_cache.shape
        n_local, _, ff = w_gate.shape
        fs = w_sh_gate.shape[1]
        kd = kvh * hd
        top = expert_ids.shape[1]
        k_t = k_cache.transpose(0, 2, 3, 1).reshape(n_rows, kd, seq)
        v_t = v_cache.transpose(0, 2, 3, 1).reshape(n_rows, kd, seq)
        cfg = (n_rows, kvh, hd, seq, n_local, tp_size, ep_size)
        half = ROWS // tp_size
        n_chunk = n_rows // ROWS
        args = (hidden, g_norm.reshape(1, d), w_q, w_k, w_v, w_o, k_t, v_t, lengths, w_sh_gate, w_sh_up, w_sh_down,
                w_gate, w_up, w_down, expert_ids.T, gate_vals.T)
        v = pltpu.VMEM
        dma = pltpu.SemaphoreType.DMA
        scratch = [
            v((4, n_rows, d), BF), v((4, n_rows, d), BF), v((1, d), F32), v(w_q.shape, BF), v(w_k.shape, BF), v(w_v.shape, BF), v(w_o.shape, BF),
            v(w_sh_gate.shape, BF), v(w_sh_up.shape, BF), v(w_sh_down.shape, BF), v(w_gate.shape, BF), v(w_up.shape, BF), v(w_down.shape, BF),
            v((4, top, n_rows), jnp.int32), v((4, top, n_rows), F32), v((4, n_local, n_rows, LANES), F32),
            v((SLOTS, TB, kd, seq), BF), v((SLOTS, TB, kd, seq), BF), pltpu.SMEM((n_rows,), jnp.int32),
            v((n_rows, kd), F32), v((n_rows, kd), F32), v((n_rows, kd), F32), v((n_rows, kd), F32), v((n_rows, 2 * kd), F32),
            v((n_rows, d), F32), v((4, n_rows, d), F32), v((n_rows, d), F32), v((n_rows, d), F32), v((n_rows, d), F32),
            v((n_chunk, half, d), F32), v((n_chunk, half, d), F32), v((ROWS, ff), BF), v((n_rows, d), BF),
            dma((12,)), dma((3,)), dma((SLOTS,)), dma((SLOTS,)), dma((n_chunk,)), dma((22,)), dma((22,)),
        ]
        return pl.pallas_call(
            functools.partial(layer_kernel, cfg),
            out_shape=jax.ShapeDtypeStruct((n_rows, d), BF),
            in_specs=[pl.BlockSpec(memory_space=pl.ANY)] * len(args),
            out_specs=pl.BlockSpec(memory_space=pl.ANY),
            scratch_shapes=scratch,
            compiler_params=pltpu.CompilerParams(collective_id=0, has_side_effects=True, vmem_limit_bytes=67043328),
            name='layer',
        )(*args)

    return jax.shard_map(device_step, mesh=mesh, in_specs=(tok_spec, P(None), col_spec, col_spec, col_spec, row_spec, cache_spec, cache_spec, P(('rep', 'ep')), col_spec, col_spec, row_spec, expert_spec, expert_spec, expert_spec, tok_spec, tok_spec), out_specs=tok_spec, check_vma=False)
```

time: 252 us -> 92.5 us (0.37)
  other arithmetic: 69.9 us -> 0 us
  Pallas kernels: 30.1 us -> 90.5 us
  waiting for transfers between devices: 49.3 us -> 0 us
  local copies, waits for them, and re-layouts: 40.6 us -> 1.87 us
  matrix products: 36.1 us -> 0 us
  between operations: 13.8 us -> 0.01 us
  starting transfers between devices: 13.6 us -> 0 us
    pallas_call x0 -> x1, Pallas kernels: none -> 90.5 us  [device_step(): pl.pallas_call(functools.partial(layer_kernel, cfg), out_shape=jax.ShapeD...]
    psum x1 -> x0, waiting for transfers between devices: 37.8 us -> none  [device_step(): total_sum = lax.psum(dense + routed, 'tp')]
    dot_general x8 -> x0, matrix products: 36.1 us -> none  [the longest x1 15.4 us: local_attention(): jnp.einsum('bkgs,bskd->bkgd', probs_bf, v_cache, preferred_element_type=j...]
    gather x4 -> x0, local copies, waits for them, and re-layouts: 34 us -> none  [the longest x1 12.8 us: device_step(): jnp.take(returned, jnp.minimum(target, n_slots - 1), axis=0)]
    another operation x3 -> x0, Pallas kernels: 28.5 us -> none
    scatter-add x2 -> x0, other arithmetic: 23 us -> none  [the longest x1 11.5 us: device_step(): jax.ops.segment_sum(flat_ids % n_local + 1, target, num_segments=n_slots)]
    reduce_sum x5 -> x0, other arithmetic: 15 us -> none  [the longest x1 6.95 us: local_attention(): prob_sum = jnp.sum(probs_f32, axis=-1) + self_prob]
    all_to_all x3 -> x0, starting transfers between devices: 13.5 us -> none  [the longest x1 4.61 us: device_step(): recv_exp = lax.all_to_all(send_exp, 'ep', 0, 0, tiled=True)]
  transfers between devices with their start and end apart: 4 -> 0, of which waited for: 3 -> 0; matrix products, arithmetic and copies ran while one was open for 30% -> 0% of each run, Pallas kernels for 1% -> 0%
where the time goes in v1:
time: 92.5 us; the launch traced here: 92.3 us
  Pallas kernels  90.5 us (98%)
  local copies, waits for them, and re-layouts  1.87 us (2%)
    pallas_call x1, Pallas kernels, device_step(): pl.pallas_call(functools.partial(layer_kernel, cfg), out_shape=jax.ShapeD...  90.5 us
    unnamed x1, local copies, waits for them, and re-layouts  1.87 us

profile of v1, /device:TPU:0, one launch (start us, length us, event | category | flops | bytes accessed | tf_op | source)
XLA Modules:
  0.0 92.3 jit_solution(2086337910885934375)
XLA Ops:
  0.0 90.5 %layer.1 = bf16[256,1024]{1,0:T(8,128)(2,1)} custom-call(bf16[256,1024]{1,0:T(8,128)(2,1)} %hid_hbm.1, f32[1,1024]{1,0:T(1,128)} %bitcast.13, bf16[1024,512]{1,0:T(8,128)(2,1)} %wq_hbm.1, bf16[1024,256]{1,0:T(8,128)(2,1)} %wk_hbm.1, bf16[1024,256]{1,0:T(8,128)(2,1)} %wv_hbm.1, bf16[512,1024]{1,0:T(8,128)(2,1)} %wo_hbm.1, bf16[256,256,256]{2,1,0:T(8,128)(2,1)} %bitcast.9, ...), custom_call_target="tpu_custom_call" | custom-call | tf_op jit(solution)/shard_map/layer/pallas_call | solution.py:335
  90.5 1.9 %copy.19 = bf16[256,1024]{1,0:T(8,128)(2,1)} copy(bf16[256,1024]{1,0:T(8,128)(2,1)} %layer.1) | data formatting | bytes 1048576

commit v2 on v1

v2 whole, which is shorter than its diff:
```python
import functools

import jax
import jax.numpy as jnp
from jax import lax
from jax.experimental import pallas as pl
from jax.experimental.pallas import tpu as pltpu
from jax.sharding import PartitionSpec as P

RMS_EPS = 1e-6
TB = 8
SLOTS = 6
ROWS = 128
SUB = 64
LANES = 128
BF = jnp.bfloat16
F32 = jnp.float32


def one_hot_mat(rows, cols, fn):
    r = lax.broadcasted_iota(jnp.int32, (rows, cols), 0)
    c = lax.broadcasted_iota(jnp.int32, (rows, cols), 1)
    return jnp.where(fn(r, c), 1.0, 0.0).astype(BF)


def dotf(a, b):
    return jnp.dot(a, b, preferred_element_type=F32)


def dot_nt(a, b):
    return lax.dot_general(a, b, (((1,), (1,)), ((), ())), preferred_element_type=F32)


def layer_kernel(cfg, hid_hbm, gn_hbm, wq_hbm, wk_hbm, wv_hbm, wo_hbm, k_hbm, v_hbm, len_hbm, wsg_hbm, wsu_hbm, wsd_hbm,
                 wg_hbm, wu_hbm, wd_hbm, ids_hbm, gts_hbm, out_hbm,
                 hall, xall, gn, wq, wk, wv, wo, wsg, wsu, wsd, wg, wu, wd, idg, gtg, gb, kbuf, vbuf, lens,
                 q0, q1, kn, vn, ctx, dense, part, rpf, rph, act, outb, qs, ss, sc, ps, sp, tf, ryf, xs, rxf, ty, ryo,
                 lsem, wsem, ksem, vsem, osem, s_send, s_recv):
    n_rows, kvh, hd, seq, n_local, tp_size, ep_size = cfg
    d_model = hall.shape[2]
    n_chunk = n_rows // ROWS
    n_sub = n_rows // SUB
    per_chunk = ROWS // SUB
    n_blk = n_rows // TB
    kd = kvh * hd
    half = SUB // tp_size
    tp = lax.axis_index('tp')
    ep = lax.axis_index('ep')
    partner = {'ep': ep + 1 - 2 * lax.rem(ep, 2)}
    xnbr = {'ep': lax.rem(ep + ep_size // 2, ep_size)}
    ynbr = {'tp': 1 - tp}

    def local(src, dst, sem):
        return pltpu.make_async_copy(src, dst, sem)

    n_remote = [0]

    def remote(src, dst, dev):
        i = n_remote[0]
        n_remote[0] += 1
        return pltpu.make_async_remote_copy(src_ref=src, dst_ref=dst, send_sem=s_send.at[i], recv_sem=s_recv.at[i],
                                            device_id=dev, device_id_type=pl.DeviceIdType.MESH)

    def rows(i):
        return pl.ds(i * ROWS, ROWS)

    def mine(s):
        return pl.ds(pl.multiple_of(s * SUB + tp * half, half), half)

    def theirs(s):
        return pl.ds(pl.multiple_of(s * SUB + (1 - tp) * half, half), half)

    hid_cp = [local(hid_hbm, hall.at[0], lsem.at[0])]
    small_cp = [local(ids_hbm, idg.at[0], lsem.at[1]), local(gts_hbm, gtg.at[0], lsem.at[2]),
                local(gn_hbm, gn, lsem.at[3]), local(len_hbm, lens, lsem.at[4])]
    qkv_cp = [local(wq_hbm, wq, lsem.at[5]), local(wk_hbm, wk, lsem.at[6]), local(wv_hbm, wv, lsem.at[7])]
    sh_cp = [local(wsg_hbm, wsg, lsem.at[8]), local(wsu_hbm, wsu, lsem.at[9]), local(wsd_hbm, wsd, lsem.at[10]),
             local(wo_hbm, wo, lsem.at[11])]
    exp_cp = [local(wg_hbm, wg, wsem.at[0]), local(wu_hbm, wu, wsem.at[1]), local(wd_hbm, wd, wsem.at[2])]

    def k_cp(b):
        slot = lax.rem(b, SLOTS)
        return local(k_hbm.at[pl.ds(b * TB, TB)], kbuf.at[slot], ksem.at[slot])

    def v_cp(b):
        slot = lax.rem(b, SLOTS)
        return local(v_hbm.at[pl.ds(b * TB, TB)], vbuf.at[slot], vsem.at[slot])

    for c in hid_cp + small_cp + qkv_cp + exp_cp:
        c.start()
    for b in range(SLOTS):
        k_cp(b).start()
        v_cp(b).start()
    for c in sh_cp:
        c.start()

    barrier = pltpu.get_barrier_semaphore()
    for dev in (partner, xnbr, ynbr):
        pl.semaphore_signal(barrier, inc=1, device_id=dev, device_id_type=pl.DeviceIdType.MESH)
    pl.semaphore_wait(barrier, 3)

    chunks = range(n_chunk)
    subs = range(n_sub)
    x_hid = [remote(hall.at[0, rows(i)], hall.at[2, rows(i)], xnbr) for i in chunks]
    p_hid = [remote(hall.at[0, rows(i)], hall.at[1, rows(i)], partner) for i in chunks]
    f_hid = [remote(hall.at[2, rows(i)], hall.at[3, rows(i)], partner) for i in chunks]
    x_idg = [remote(idg.at[0], idg.at[2], xnbr), remote(gtg.at[0], gtg.at[2], xnbr)]
    p_idg = [remote(idg.at[0], idg.at[1], partner), remote(gtg.at[0], gtg.at[1], partner)]
    f_idg = [remote(idg.at[2], idg.at[3], partner), remote(gtg.at[2], gtg.at[3], partner)]
    c_far = [remote(part.at[3, rows(i)], rpf.at[rows(i)], partner) for i in chunks]
    c_near = [remote(part.at[1, rows(i)], rph.at[rows(i)], partner) for i in chunks]
    y_far = [remote(tf.at[s], ryf.at[s], ynbr) for s in subs]
    x_ret = [remote(xs.at[s], rxf.at[s], xnbr) for s in subs]
    y_own = [remote(ty.at[s], ryo.at[s], ynbr) for s in subs]
    y_out = [remote(outb.at[mine(s)], outb.at[mine(s)], ynbr) for s in subs]

    for c in small_cp:
        c.wait()
    for c in x_idg + p_idg:
        c.start()
    for c in hid_cp:
        c.wait()
    for c in x_hid + p_hid:
        c.start()

    def normalize(grp, r0, n):
        def body(j, carry):
            at = pl.ds(pl.multiple_of(r0 + j * 32, 32), 32)
            h32 = hall[grp, at, :].astype(F32)
            inv = lax.rsqrt(jnp.mean(h32 * h32, axis=-1, keepdims=True) + RMS_EPS)
            xall[grp, at, :] = (h32 * inv * gn[...]).astype(BF)
            return carry
        lax.fori_loop(0, n // 32, body, 0)

    first_exp = (ep * tp_size + tp) * n_local

    def gate_table(grp):
        ids = idg[grp]
        vals = gtg[grp]
        picked = [jnp.sum(jnp.where(ids == first_exp + e, vals, 0.0), axis=0, keepdims=True) for e in range(n_local)]
        table = jnp.concatenate(picked + [jnp.zeros((LANES - n_local, n_rows), F32)], axis=0)
        cols = jnp.transpose(table)
        for e in range(n_local):
            gb[grp, e] = jnp.broadcast_to(cols[:, e:e + 1], (n_rows, LANES))

    R = TB * 2 * kvh
    per_tok = 2 * kvh
    expand_q = one_hot_mat(R, 2 * TB, lambda r, c: c == ((r % per_tok) // kvh) * TB + r // per_tok)
    expand_n = one_hot_mat(R, TB, lambda r, c: c == r // per_tok)
    gather_o = one_hot_mat(2 * TB, R, lambda r, c: (c // per_tok == r % TB) & ((c % per_tok) // kvh == r // TB))
    rr = lax.broadcasted_iota(jnp.int32, (R, kd), 0)
    cc = lax.broadcasted_iota(jnp.int32, (R, kd), 1)
    own = (rr % kvh) == (cc // hd)
    pos = lax.broadcasted_iota(jnp.int32, (per_tok, seq), 1)
    scale = hd ** -0.5

    def toks(b):
        return pl.ds(pl.multiple_of(b * TB, TB), TB)

    def stage_q(b, p):
        tok = toks(b)
        qq = jnp.concatenate([q0[tok, :], q1[tok, :]], axis=0).astype(BF)
        qs[p] = jnp.where(own, dotf(expand_q, qq), 0.0)

    def heads(t):
        return slice(t * per_tok, (t + 1) * per_tok)

    def stage_kv(b, p, with_v=True, with_k=True):
        if with_k:
            k_slot = lax.rem(b, SLOTS)
            k_self = dotf(expand_n, kn[toks(b), :].astype(BF))
            ss[p] = jnp.broadcast_to(jnp.sum(qs[p] * k_self, axis=-1, keepdims=True) * scale, (R, LANES))
        if with_v:
            v_slot = lax.rem(b - 2, SLOTS)
            v_self = dotf(expand_n, vn[toks(b - 2), :].astype(BF))
        outs = []
        for t in range(TB):
            if with_k:
                s_t = dotf(qs[p, heads(t), :].astype(BF), kbuf[k_slot, t])
                sc[p, heads(t), :] = jnp.where(pos < lens[b * TB + t], s_t * scale, -1e30)
            if with_v:
                outs.append(dot_nt(ps[p, heads(t), :].astype(BF), vbuf[v_slot, t]))
        if with_v:
            o = jnp.concatenate(outs, axis=0) + jnp.concatenate([sp[p]] * (kd // LANES), axis=1) * v_self
            o2 = dotf(gather_o, jnp.where(own, o, 0.0).astype(BF))
            ctx[toks(b - 2), 0:kd] = o2[0:TB]
            ctx[toks(b - 2), kd:2 * kd] = o2[TB:2 * TB]

    def stage_s(p):
        scores = sc[p]
        self_score = ss[p, :, 0:1]
        peak = jnp.maximum(jnp.max(scores, axis=-1, keepdims=True), self_score)
        prob = jnp.exp(scores - peak)
        self_prob = jnp.exp(self_score - peak)
        inv = 1.0 / (jnp.sum(prob, axis=-1, keepdims=True) + self_prob)
        ps[p] = prob * inv
        sp[p] = jnp.broadcast_to((self_prob * inv).astype(BF).astype(F32), (R, LANES))

    def attn_pair(j, carry):
        b = 2 * j
        for p in range(2):
            k_cp(b + p).wait()
            v_cp(b + p - 2).wait()
        for p in range(2):
            stage_kv(b + p, p)
            stage_s(1 - p)
            stage_q(jnp.minimum(b + p + 1, n_blk - 1), 1 - p)
        for p in range(2):
            @pl.when(b + p + SLOTS < n_blk)
            def _():
                k_cp(b + p + SLOTS).start()

            @pl.when(b + p - 2 + SLOTS < n_blk)
            def _():
                v_cp(b + p - 2 + SLOTS).start()
        return carry

    done = [0]

    def attend(hi):
        lo = done[0]
        done[0] = hi
        if lo == 0:
            for p in range(2):
                k_cp(p).wait()
                stage_q(p, p)
            for p in range(2):
                stage_kv(p, p, with_v=False)
            stage_s(0)
            stage_q(2, 0)
            for p in range(2):
                k_cp(p + SLOTS).start()
            lo = 2
        lax.fori_loop(lo // 2, hi // 2, attn_pair, 0)
        if hi == n_blk:
            for p in range(2):
                v_cp(n_blk - 2 + p).wait()
            stage_kv(n_blk, 0, with_k=False)
            stage_s(1)
            stage_kv(n_blk + 1, 1, with_k=False)

    ff = wg.shape[2]

    def unit(g0, i):
        at = rows(i)
        m2 = 2 * ROWS

        def body(e, carry):
            xr = xall[g0:g0 + 2, at, :].reshape(m2, d_model)
            for j in range(ff // 256):
                cs = slice(j * 256, (j + 1) * 256)
                g_a = dotf(xr, wg[e, :, cs])
                u_b = dotf(xr, wu[e, :, cs])
                act[:, cs] = (g_a * jax.nn.sigmoid(g_a) * u_b).astype(BF)
            gate = gb[g0:g0 + 2, e, at, :].reshape(m2, LANES)
            hit = gate > 0.0
            first = e == 0
            for j in range(d_model // 256):
                y = dotf(act[...], wd[e, :, j * 256:(j + 1) * 256]).astype(BF).astype(F32)
                for m in range(256 // LANES):
                    ls = slice(j * 256 + m * LANES, j * 256 + (m + 1) * LANES)
                    add = jnp.where(hit, gate * y[:, m * LANES:(m + 1) * LANES], 0.0).reshape(2, ROWS, LANES)
                    part[g0:g0 + 2, at, ls] = jnp.where(first, add, part[g0:g0 + 2, at, ls] + add)
            return carry

        lax.fori_loop(0, n_local, body, 0)

    def sub_of(i):
        return range(i * per_chunk, (i + 1) * per_chunk)

    def far_y(i):
        c_far[i].wait_recv()
        for s in sub_of(i):
            at = theirs(s)
            tf[s] = part[2, at, :] + rpf[at, :]
            y_far[s].start()

    def far_x(i):
        for s in sub_of(i):
            y_far[s].wait_recv()
            at = mine(s)
            xs[s] = part[2, at, :] + rpf[at, :] + ryf[s]
            x_ret[s].start()

    def arrive(i):
        x_hid[i].wait_recv()
        f_hid[i].start()
        normalize(2, i * ROWS, ROWS)

    def far(i):
        f_hid[i].wait_recv()
        normalize(3, i * ROWS, ROWS)
        unit(2, i)
        c_far[i].start()

    def near(i):
        p_hid[i].wait_recv()
        normalize(1, i * ROWS, ROWS)
        unit(0, i)
        c_near[i].start()

    def shared_expert():
        for c in sh_cp:
            c.wait()
        sg = dotf(xall[0], wsg[...])
        su = dotf(xall[0], wsu[...])
        sa = (sg * jax.nn.sigmoid(sg) * su).astype(BF)
        for j in range(d_model // 256):
            cs = slice(j * 256, (j + 1) * 256)
            dense[:, cs] = dotf(sa, wsd[:, cs])

    swap = one_hot_mat(2 * kd, 2 * kd, lambda r, c: ((r // kd) == ((c // hd) % 2)) & ((r % kd) // hd == c // (2 * hd)) & (r % hd == c % hd))

    def own_y(s):
        if s % per_chunk == 0:
            c_near[s // per_chunk].wait_recv()
        at = pl.ds(s * SUB, SUB)
        ctx_bf = dotf(ctx[at, :].astype(BF), swap).astype(BF)
        for j in range(d_model // 256):
            cs = slice(j * 256, (j + 1) * 256)
            dense[at, cs] = dense[at, cs] + dotf(ctx_bf, wo[:, cs]) + part[0, at, cs] + rph[at, cs]
        ty[s] = dense[theirs(s), :]
        y_own[s].start()

    def finish(s):
        y_own[s].wait_recv()
        x_ret[s].wait_recv()
        at = mine(s)
        outb[at, :] = (hall[0, at, :].astype(F32) + (dense[at, :] + ryo[s] + rxf[s])).astype(BF)
        y_out[s].start()

    normalize(0, 0, n_rows)
    for c in qkv_cp:
        c.wait()

    nq = wq.shape[1]
    q_bf = [dotf(xall[0], wq[:, j * 256:(j + 1) * 256]).astype(BF) for j in range(nq // 256)]
    for g, ref in enumerate((q0, q1)):
        acc = None
        for j in range(nq // 256):
            def sel(r, c, j=j, g=g):
                r2 = r + j * 256
                return ((r2 // (2 * hd)) == (c // hd)) & ((r2 % (2 * hd)) == g * hd + c % hd)
            term = dotf(q_bf[j], one_hot_mat(256, kd, sel))
            acc = term if acc is None else acc + term
        ref[...] = acc
    kn[...] = dotf(xall[0], wk[...]).astype(BF).astype(F32)
    vn[...] = dotf(xall[0], wv[...]).astype(BF).astype(F32)

    for c in p_idg:
        c.wait_recv()
    gate_table(0)
    gate_table(1)
    for c in exp_cp:
        c.wait()
    near(0)
    attend(4)
    for c in x_idg:
        c.wait_recv()
    for c in f_idg:
        c.start()
    arrive(0)
    gate_table(2)
    attend(6)
    for c in f_idg:
        c.wait_recv()
    gate_table(3)
    far(0)
    attend(8)
    far_y(0)
    near(1)
    arrive(1)
    attend(10)
    far(1)
    shared_expert()
    attend(12)
    far_y(1)
    own_y(0)
    attend(14)
    far_x(0)
    attend(18)
    own_y(1)
    attend(20)
    far_x(1)
    attend(26)
    own_y(2)
    finish(0)
    attend(28)
    finish(1)
    attend(n_blk)
    own_y(3)
    finish(2)
    finish(3)
    out_cp = []
    for s in subs:
        y_out[s].wait_recv()
        at = pl.ds(s * SUB, SUB)
        c = local(outb.at[at], out_hbm.at[at], osem.at[s])
        c.start()
        out_cp.append(c)
    for c in x_hid + p_hid + f_hid + x_idg + p_idg + f_idg + c_far + c_near + y_far + x_ret + y_own + y_out:
        c.wait_send()
    for c in out_cp:
        c.wait()


def solution(mesh):
    tp_size = mesh.shape['tp']
    ep_size = mesh.shape['ep']
    tok_spec = P(('rep', 'ep'), None)
    col_spec = P(None, 'tp')
    row_spec = P('tp', None)
    cache_spec = P(('rep', 'ep'), None, 'tp', None)
    expert_spec = P(('ep', 'tp'), None, None)

    def device_step(hidden, g_norm, w_q, w_k, w_v, w_o, k_cache, v_cache, lengths, w_sh_gate, w_sh_up, w_sh_down, w_gate, w_up, w_down, expert_ids, gate_vals):
        n_rows, d = hidden.shape
        _, seq, kvh, hd = k_cache.shape
        n_local, _, ff = w_gate.shape
        fs = w_sh_gate.shape[1]
        kd = kvh * hd
        top = expert_ids.shape[1]
        k_t = k_cache.transpose(0, 2, 3, 1).reshape(n_rows, kd, seq)
        v_t = v_cache.transpose(0, 2, 3, 1).reshape(n_rows, kd, seq)
        cfg = (n_rows, kvh, hd, seq, n_local, tp_size, ep_size)
        half = SUB // tp_size
        n_chunk = n_rows // ROWS
        n_sub = n_rows // SUB
        n_remote = 5 * n_chunk + 6 + 4 * n_sub
        R = TB * 2 * kvh
        args = (hidden, g_norm.reshape(1, d), w_q, w_k, w_v, w_o, k_t, v_t, lengths, w_sh_gate, w_sh_up, w_sh_down,
                w_gate, w_up, w_down, expert_ids.T, gate_vals.T)
        v = pltpu.VMEM
        dma = pltpu.SemaphoreType.DMA
        scratch = [
            v((4, n_rows, d), BF), v((4, n_rows, d), BF), v((1, d), F32), v(w_q.shape, BF), v(w_k.shape, BF), v(w_v.shape, BF), v(w_o.shape, BF),
            v(w_sh_gate.shape, BF), v(w_sh_up.shape, BF), v(w_sh_down.shape, BF), v(w_gate.shape, BF), v(w_up.shape, BF), v(w_down.shape, BF),
            v((4, top, n_rows), jnp.int32), v((4, top, n_rows), F32), v((4, n_local, n_rows, LANES), F32),
            v((SLOTS, TB, kd, seq), BF), v((SLOTS, TB, kd, seq), BF), pltpu.SMEM((n_rows,), jnp.int32),
            v((n_rows, kd), F32), v((n_rows, kd), F32), v((n_rows, kd), F32), v((n_rows, kd), F32), v((n_rows, 2 * kd), F32),
            v((n_rows, d), F32), v((4, n_rows, d), F32), v((n_rows, d), F32), v((n_rows, d), F32), v((2 * ROWS, ff), BF), v((n_rows, d), BF),
            v((2, R, kd), F32), v((2, R, LANES), F32), v((2, R, seq), F32), v((2, R, seq), F32), v((2, R, LANES), F32),
            *[v((n_sub, half, d), F32)] * 6,
            dma((12,)), dma((3,)), dma((SLOTS,)), dma((SLOTS,)), dma((n_sub,)), dma((n_remote,)), dma((n_remote,)),
        ]
        return pl.pallas_call(
            functools.partial(layer_kernel, cfg),
            out_shape=jax.ShapeDtypeStruct((n_rows, d), BF),
            in_specs=[pl.BlockSpec(memory_space=pl.ANY)] * len(args),
            out_specs=pl.BlockSpec(memory_space=pl.ANY),
            scratch_shapes=scratch,
            compiler_params=pltpu.CompilerParams(collective_id=0, has_side_effects=True, vmem_limit_bytes=67043328),
            name='layer',
        )(*args)

    return jax.shard_map(device_step, mesh=mesh, in_specs=(tok_spec, P(None), col_spec, col_spec, col_spec, row_spec, cache_spec, cache_spec, P(('rep', 'ep')), col_spec, col_spec, row_spec, expert_spec, expert_spec, expert_spec, tok_spec, tok_spec), out_specs=tok_spec, check_vma=False)
```

time: 92.5 us -> 70.2 us (0.76)
  Pallas kernels: 90.5 us -> 68.2 us
    pallas_call x1, Pallas kernels: 90.5 us -> 68.2 us  [device_step(): pl.pallas_call(functools.partial(layer_kernel, cfg), out_shape=jax.ShapeD...]
where the time goes in v2:
time: 70.2 us; the launch traced here: 70.1 us
  Pallas kernels  68.2 us (97%)
  local copies, waits for them, and re-layouts  1.87 us (3%)
    pallas_call x1, Pallas kernels, device_step(): pl.pallas_call(functools.partial(layer_kernel, cfg), out_shape=jax.ShapeD...  68.2 us
    unnamed x1, local copies, waits for them, and re-layouts  1.87 us

profile of v2, /device:TPU:0, one launch (start us, length us, event | category | flops | bytes accessed | tf_op | source)
XLA Modules:
  0.0 70.1 jit_solution(1995768306417515988)
XLA Ops:
  0.0 68.2 %layer.1 = bf16[256,1024]{1,0:T(8,128)(2,1)} custom-call(bf16[256,1024]{1,0:T(8,128)(2,1)} %hid_hbm.1, f32[1,1024]{1,0:T(1,128)} %bitcast.13, bf16[1024,512]{1,0:T(8,128)(2,1)} %wq_hbm.1, bf16[1024,256]{1,0:T(8,128)(2,1)} %wk_hbm.1, bf16[1024,256]{1,0:T(8,128)(2,1)} %wv_hbm.1, bf16[512,1024]{1,0:T(8,128)(2,1)} %wo_hbm.1, bf16[256,256,256]{2,1,0:T(8,128)(2,1)} %bitcast.9, ...), custom_call_target="tpu_custom_call" | custom-call | tf_op jit(solution)/shard_map/layer/pallas_call | solution.py:446
  68.2 1.9 %copy.19 = bf16[256,1024]{1,0:T(8,128)(2,1)} copy(bf16[256,1024]{1,0:T(8,128)(2,1)} %layer.1) | data formatting | bytes 1048576

commit v3 on v2

--- a/solution.py
+++ b/solution.py
@@ -9,9 +9,10 @@
 
 RMS_EPS = 1e-6
 TB = 8
-SLOTS = 6
+EARLY = 6
+SLOTS = 8
 ROWS = 128
-SUB = 64
+SUBS = ((0, 64), (64, 64), (128, 64), (192, 32), (224, 32))
 LANES = 128
 BF = jnp.bfloat16
 F32 = jnp.float32
@@ -34,16 +35,13 @@
 def layer_kernel(cfg, hid_hbm, gn_hbm, wq_hbm, wk_hbm, wv_hbm, wo_hbm, k_hbm, v_hbm, len_hbm, wsg_hbm, wsu_hbm, wsd_hbm,
                  wg_hbm, wu_hbm, wd_hbm, ids_hbm, gts_hbm, out_hbm,
                  hall, xall, gn, wq, wk, wv, wo, wsg, wsu, wsd, wg, wu, wd, idg, gtg, gb, kbuf, vbuf, lens,
-                 q0, q1, kn, vn, ctx, dense, part, rpf, rph, act, outb, qs, ss, sc, ps, sp, tf, ryf, xs, rxf, ty, ryo,
+                 q0, q1, kn, vn, om, dense, part, rpf, rph, act, outb, ss, sc, ps, sp, tf, ryf, xs, rxf, ty, ryo,
                  lsem, wsem, ksem, vsem, osem, s_send, s_recv):
     n_rows, kvh, hd, seq, n_local, tp_size, ep_size = cfg
     d_model = hall.shape[2]
     n_chunk = n_rows // ROWS
-    n_sub = n_rows // SUB
-    per_chunk = ROWS // SUB
     n_blk = n_rows // TB
     kd = kvh * hd
-    half = SUB // tp_size
     tp = lax.axis_index('tp')
     ep = lax.axis_index('ep')
     partner = {'ep': ep + 1 - 2 * lax.rem(ep, 2)}
@@ -65,10 +63,16 @@
         return pl.ds(i * ROWS, ROWS)
 
     def mine(s):
-        return pl.ds(pl.multiple_of(s * SUB + tp * half, half), half)
+        r0, n = SUBS[s]
+        return pl.ds(pl.multiple_of(r0 + tp * (n // 2), n // 2), n // 2)
 
     def theirs(s):
-        return pl.ds(pl.multiple_of(s * SUB + (1 - tp) * half, half), half)
+        r0, n = SUBS[s]
+        return pl.ds(pl.multiple_of(r0 + (1 - tp) * (n // 2), n // 2), n // 2)
+
+    def packed(s):
+        r0, n = SUBS[s]
+        return pl.ds(r0 // 2, n // 2)
 
     hid_cp = [local(hid_hbm, hall.at[0], lsem.at[0])]
     small_cp = [local(ids_hbm, idg.at[0], lsem.at[1]), local(gts_hbm, gtg.at[0], lsem.at[2]),
@@ -86,9 +90,14 @@
         slot = lax.rem(b, SLOTS)
         return local(v_hbm.at[pl.ds(b * TB, TB)], vbuf.at[slot], vsem.at[slot])
 
-    for c in hid_cp + small_cp + qkv_cp + exp_cp:
-        c.start()
-    for b in range(SLOTS):
+    for c in hid_cp + small_cp + qkv_cp:
+        c.start()
+    for b in range(EARLY):
+        k_cp(b).start()
+        v_cp(b).start()
+    for c in exp_cp:
+        c.start()
+    for b in range(EARLY, SLOTS):
         k_cp(b).start()
         v_cp(b).start()
     for c in sh_cp:
@@ -100,7 +109,7 @@
     pl.semaphore_wait(barrier, 3)
 
     chunks = range(n_chunk)
-    subs = range(n_sub)
+    subs = range(len(SUBS))
     x_hid = [remote(hall.at[0, rows(i)], hall.at[2, rows(i)], xnbr) for i in chunks]
     p_hid = [remote(hall.at[0, rows(i)], hall.at[1, rows(i)], partner) for i in chunks]
     f_hid = [remote(hall.at[2, rows(i)], hall.at[3, rows(i)], partner) for i in chunks]
@@ -109,9 +118,9 @@
     f_idg = [remote(idg.at[2], idg.at[3], partner), remote(gtg.at[2], gtg.at[3], partner)]
     c_far = [remote(part.at[3, rows(i)], rpf.at[rows(i)], partner) for i in chunks]
     c_near = [remote(part.at[1, rows(i)], rph.at[rows(i)], partner) for i in chunks]
-    y_far = [remote(tf.at[s], ryf.at[s], ynbr) for s in subs]
-    x_ret = [remote(xs.at[s], rxf.at[s], xnbr) for s in subs]
-    y_own = [remote(ty.at[s], ryo.at[s], ynbr) for s in subs]
+    y_far = [remote(tf.at[packed(s)], ryf.at[packed(s)], ynbr) for s in subs]
+    x_ret = [remote(xs.at[packed(s)], rxf.at[packed(s)], xnbr) for s in subs]
+    y_own = [remote(ty.at[packed(s)], ryo.at[packed(s)], ynbr) for s in subs]
     y_out = [remote(outb.at[mine(s)], outb.at[mine(s)], ynbr) for s in subs]
 
     for c in small_cp:
@@ -143,48 +152,35 @@
         for e in range(n_local):
             gb[grp, e] = jnp.broadcast_to(cols[:, e:e + 1], (n_rows, LANES))
 
-    R = TB * 2 * kvh
     per_tok = 2 * kvh
-    expand_q = one_hot_mat(R, 2 * TB, lambda r, c: c == ((r % per_tok) // kvh) * TB + r // per_tok)
-    expand_n = one_hot_mat(R, TB, lambda r, c: c == r // per_tok)
-    gather_o = one_hot_mat(2 * TB, R, lambda r, c: (c // per_tok == r % TB) & ((c % per_tok) // kvh == r // TB))
-    rr = lax.broadcasted_iota(jnp.int32, (R, kd), 0)
-    cc = lax.broadcasted_iota(jnp.int32, (R, kd), 1)
+    R = TB * per_tok
+    rr = lax.broadcasted_iota(jnp.int32, (per_tok, kd), 0)
+    cc = lax.broadcasted_iota(jnp.int32, (per_tok, kd), 1)
     own = (rr % kvh) == (cc // hd)
+    low = rr < kvh
     pos = lax.broadcasted_iota(jnp.int32, (per_tok, seq), 1)
     scale = hd ** -0.5
 
-    def toks(b):
-        return pl.ds(pl.multiple_of(b * TB, TB), TB)
-
-    def stage_q(b, p):
-        tok = toks(b)
-        qq = jnp.concatenate([q0[tok, :], q1[tok, :]], axis=0).astype(BF)
-        qs[p] = jnp.where(own, dotf(expand_q, qq), 0.0)
-
     def heads(t):
         return slice(t * per_tok, (t + 1) * per_tok)
 
+    def spread(ref, tok):
+        return jnp.broadcast_to(ref[pl.ds(tok, 1), :], (per_tok, kd))
+
     def stage_kv(b, p, with_v=True, with_k=True):
-        if with_k:
-            k_slot = lax.rem(b, SLOTS)
-            k_self = dotf(expand_n, kn[toks(b), :].astype(BF))
-            ss[p] = jnp.broadcast_to(jnp.sum(qs[p] * k_self, axis=-1, keepdims=True) * scale, (R, LANES))
-        if with_v:
-            v_slot = lax.rem(b - 2, SLOTS)
-            v_self = dotf(expand_n, vn[toks(b - 2), :].astype(BF))
-        outs = []
         for t in range(TB):
             if with_k:
-                s_t = dotf(qs[p, heads(t), :].astype(BF), kbuf[k_slot, t])
-                sc[p, heads(t), :] = jnp.where(pos < lens[b * TB + t], s_t * scale, -1e30)
+                tok = b * TB + t
+                q_t = jnp.where(own, jnp.where(low, spread(q0, tok), spread(q1, tok)), 0.0)
+                s_t = dotf(q_t.astype(BF), kbuf[lax.rem(b, SLOTS), t])
+                sc[p, heads(t), :] = jnp.where(pos < lens[tok], s_t * scale, -1e30)
+                self_t = jnp.sum(q_t * spread(kn, tok), axis=-1, keepdims=True) * scale
+                ss[p, heads(t), :] = jnp.broadcast_to(self_t, (per_tok, LANES))
             if with_v:
-                outs.append(dot_nt(ps[p, heads(t), :].astype(BF), vbuf[v_slot, t]))
-        if with_v:
-            o = jnp.concatenate(outs, axis=0) + jnp.concatenate([sp[p]] * (kd // LANES), axis=1) * v_self
-            o2 = dotf(gather_o, jnp.where(own, o, 0.0).astype(BF))
-            ctx[toks(b - 2), 0:kd] = o2[0:TB]
-            ctx[toks(b - 2), kd:2 * kd] = o2[TB:2 * TB]
+                tok = (b - 2) * TB + t
+                o_t = dot_nt(ps[p, heads(t), :].astype(BF), vbuf[lax.rem(b - 2, SLOTS), t])
+                o_t = o_t + jnp.concatenate([sp[p, heads(t), :]] * (kd // LANES), axis=1) * spread(vn, tok)
+                om[pl.ds(pl.multiple_of(tok * per_tok, per_tok), per_tok), :] = jnp.where(own, o_t, 0.0)
 
     def stage_s(p):
         scores = sc[p]
@@ -204,7 +200,6 @@
         for p in range(2):
             stage_kv(b + p, p)
             stage_s(1 - p)
-            stage_q(jnp.minimum(b + p + 1, n_blk - 1), 1 - p)
         for p in range(2):
             @pl.when(b + p + SLOTS < n_blk)
             def _():
@@ -223,11 +218,9 @@
         if lo == 0:
             for p in range(2):
                 k_cp(p).wait()
-                stage_q(p, p)
             for p in range(2):
                 stage_kv(p, p, with_v=False)
             stage_s(0)
-            stage_q(2, 0)
             for p in range(2):
                 k_cp(p + SLOTS).start()
             lo = 2
@@ -241,45 +234,51 @@
 
     ff = wg.shape[2]
 
-    def unit(g0, i):
-        at = rows(i)
-        m2 = 2 * ROWS
-
-        def body(e, carry):
-            xr = xall[g0:g0 + 2, at, :].reshape(m2, d_model)
-            for j in range(ff // 256):
-                cs = slice(j * 256, (j + 1) * 256)
-                g_a = dotf(xr, wg[e, :, cs])
-                u_b = dotf(xr, wu[e, :, cs])
-                act[:, cs] = (g_a * jax.nn.sigmoid(g_a) * u_b).astype(BF)
+    def unit(g0, r0, n):
+        at = pl.ds(r0, n)
+        m2 = 2 * n
+
+        xr = xall[g0:g0 + 2, at, :].reshape(m2, d_model)
+
+        def up(e, j):
+            cs = slice(j * 256, (j + 1) * 256)
+            g_a = dotf(xr, wg[e, :, cs])
+            u_b = dotf(xr, wu[e, :, cs])
+            act[e % 2, :, cs] = (g_a * jax.nn.sigmoid(g_a) * u_b).astype(BF)
+
+        def down(e, j):
             gate = gb[g0:g0 + 2, e, at, :].reshape(m2, LANES)
-            hit = gate > 0.0
-            first = e == 0
-            for j in range(d_model // 256):
-                y = dotf(act[...], wd[e, :, j * 256:(j + 1) * 256]).astype(BF).astype(F32)
-                for m in range(256 // LANES):
-                    ls = slice(j * 256 + m * LANES, j * 256 + (m + 1) * LANES)
-                    add = jnp.where(hit, gate * y[:, m * LANES:(m + 1) * LANES], 0.0).reshape(2, ROWS, LANES)
-                    part[g0:g0 + 2, at, ls] = jnp.where(first, add, part[g0:g0 + 2, at, ls] + add)
-            return carry
-
-        lax.fori_loop(0, n_local, body, 0)
+            y = dotf(act[e % 2], wd[e, :, j * 256:(j + 1) * 256]).astype(BF).astype(F32)
+            for m in range(256 // LANES):
+                ls = slice(j * 256 + m * LANES, j * 256 + (m + 1) * LANES)
+                add = jnp.where(gate > 0.0, gate * y[:, m * LANES:(m + 1) * LANES], 0.0).reshape(2, n, LANES)
+                part[g0:g0 + 2, at, ls] = add if e == 0 else part[g0:g0 + 2, at, ls] + add
+
+        n_up = ff // 256
+        n_down = d_model // 256
+        for e in range(n_local + 1):
+            for j in range(n_up):
+                if e < n_local:
+                    up(e, j)
+                if e > 0:
+                    for k in range(j * n_down // n_up, (j + 1) * n_down // n_up):
+                        down(e - 1, k)
 
     def sub_of(i):
-        return range(i * per_chunk, (i + 1) * per_chunk)
+        return [s for s in subs if SUBS[s][0] // ROWS == i]
 
     def far_y(i):
         c_far[i].wait_recv()
         for s in sub_of(i):
             at = theirs(s)
-            tf[s] = part[2, at, :] + rpf[at, :]
+            tf[packed(s), :] = part[2, at, :] + rpf[at, :]
             y_far[s].start()
 
     def far_x(i):
         for s in sub_of(i):
             y_far[s].wait_recv()
             at = mine(s)
-            xs[s] = part[2, at, :] + rpf[at, :] + ryf[s]
+            xs[packed(s), :] = part[2, at, :] + rpf[at, :] + ryf[packed(s), :]
             x_ret[s].start()
 
     def arrive(i):
@@ -290,13 +289,13 @@
     def far(i):
         f_hid[i].wait_recv()
         normalize(3, i * ROWS, ROWS)
-        unit(2, i)
+        unit(2, i * ROWS, ROWS)
         c_far[i].start()
 
     def near(i):
         p_hid[i].wait_recv()
         normalize(1, i * ROWS, ROWS)
-        unit(0, i)
+        unit(0, i * ROWS, ROWS)
         c_near[i].start()
 
     def shared_expert():
@@ -312,21 +311,24 @@
     swap = one_hot_mat(2 * kd, 2 * kd, lambda r, c: ((r // kd) == ((c // hd) % 2)) & ((r % kd) // hd == c // (2 * hd)) & (r % hd == c % hd))
 
     def own_y(s):
-        if s % per_chunk == 0:
-            c_near[s // per_chunk].wait_recv()
-        at = pl.ds(s * SUB, SUB)
-        ctx_bf = dotf(ctx[at, :].astype(BF), swap).astype(BF)
+        r0, n = SUBS[s]
+        if s in (sub_of(0)[0], sub_of(1)[0]):
+            c_near[r0 // ROWS].wait_recv()
+        at = pl.ds(r0, n)
+        gather_o = one_hot_mat(2 * n, n * per_tok, lambda r, c: (c // per_tok == r % n) & ((c % per_tok) // kvh == r // n))
+        o2 = dotf(gather_o, om[pl.ds(r0 * per_tok, n * per_tok), :].astype(BF)).astype(BF)
+        ctx_bf = dotf(jnp.concatenate([o2[0:n], o2[n:2 * n]], axis=1), swap).astype(BF)
         for j in range(d_model // 256):
             cs = slice(j * 256, (j + 1) * 256)
             dense[at, cs] = dense[at, cs] + dotf(ctx_bf, wo[:, cs]) + part[0, at, cs] + rph[at, cs]
-        ty[s] = dense[theirs(s), :]
+        ty[packed(s), :] = dense[theirs(s), :]
         y_own[s].start()
 
     def finish(s):
         y_own[s].wait_recv()
         x_ret[s].wait_recv()
         at = mine(s)
-        outb[at, :] = (hall[0, at, :].astype(F32) + (dense[at, :] + ryo[s] + rxf[s])).astype(BF)
+        outb[at, :] = (hall[0, at, :].astype(F32) + (dense[at, :] + ryo[packed(s), :] + rxf[packed(s), :])).astype(BF)
         y_out[s].start()
 
     normalize(0, 0, n_rows)
@@ -347,54 +349,52 @@
     kn[...] = dotf(xall[0], wk[...]).astype(BF).astype(F32)
     vn[...] = dotf(xall[0], wv[...]).astype(BF).astype(F32)
 
-    for c in p_idg:
+    attend(8)
+    for c in p_idg + x_idg:
         c.wait_recv()
+    for c in f_idg:
+        c.start()
     gate_table(0)
     gate_table(1)
+    gate_table(2)
+    attend(10)
+    arrive(0)
     for c in exp_cp:
         c.wait()
-    near(0)
-    attend(4)
-    for c in x_idg:
-        c.wait_recv()
-    for c in f_idg:
-        c.start()
-    arrive(0)
-    gate_table(2)
-    attend(6)
+    attend(12)
     for c in f_idg:
         c.wait_recv()
     gate_table(3)
     far(0)
-    attend(8)
+    arrive(1)
+    attend(14)
     far_y(0)
+    far(1)
+    attend(18)
+    far_y(1)
+    near(0)
+    shared_expert()
+    far_x(0)
     near(1)
-    arrive(1)
-    attend(10)
-    far(1)
-    shared_expert()
-    attend(12)
-    far_y(1)
     own_y(0)
-    attend(14)
-    far_x(0)
-    attend(18)
     own_y(1)
-    attend(20)
+    attend(22)
     far_x(1)
     attend(26)
     own_y(2)
     finish(0)
-    attend(28)
     finish(1)
-    attend(n_blk)
+    attend(30)
     own_y(3)
     finish(2)
+    attend(n_blk)
+    own_y(4)
     finish(3)
+    finish(4)
     out_cp = []
     for s in subs:
         y_out[s].wait_recv()
-        at = pl.ds(s * SUB, SUB)
+        at = pl.ds(*SUBS[s])
         c = local(outb.at[at], out_hbm.at[at], osem.at[s])
         c.start()
         out_cp.append(c)
@@ -423,9 +423,8 @@
         k_t = k_cache.transpose(0, 2, 3, 1).reshape(n_rows, kd, seq)
         v_t = v_cache.transpose(0, 2, 3, 1).reshape(n_rows, kd, seq)
         cfg = (n_rows, kvh, hd, seq, n_local, tp_size, ep_size)
-        half = SUB // tp_size
         n_chunk = n_rows // ROWS
-        n_sub = n_rows // SUB
+        n_sub = len(SUBS)
         n_remote = 5 * n_chunk + 6 + 4 * n_sub
         R = TB * 2 * kvh
         args = (hidden, g_norm.reshape(1, d), w_q, w_k, w_v, w_o, k_t, v_t, lengths, w_sh_gate, w_sh_up, w_sh_down,
@@ -437,10 +436,10 @@
             v(w_sh_gate.shape, BF), v(w_sh_up.shape, BF), v(w_sh_down.shape, BF), v(w_gate.shape, BF), v(w_up.shape, BF), v(w_down.shape, BF),
             v((4, top, n_rows), jnp.int32), v((4, top, n_rows), F32), v((4, n_local, n_rows, LANES), F32),
             v((SLOTS, TB, kd, seq), BF), v((SLOTS, TB, kd, seq), BF), pltpu.SMEM((n_rows,), jnp.int32),
-            v((n_rows, kd), F32), v((n_rows, kd), F32), v((n_rows, kd), F32), v((n_rows, kd), F32), v((n_rows, 2 * kd), F32),
-            v((n_rows, d), F32), v((4, n_rows, d), F32), v((n_rows, d), F32), v((n_rows, d), F32), v((2 * ROWS, ff), BF), v((n_rows, d), BF),
-            v((2, R, kd), F32), v((2, R, LANES), F32), v((2, R, seq), F32), v((2, R, seq), F32), v((2, R, LANES), F32),
-            *[v((n_sub, half, d), F32)] * 6,
+            v((n_rows, kd), F32), v((n_rows, kd), F32), v((n_rows, kd), F32), v((n_rows, kd), F32), v((n_rows * 2 * kvh, kd), F32),
+            v((n_rows, d), F32), v((4, n_rows, d), F32), v((n_rows, d), F32), v((n_rows, d), F32), v((2, 2 * ROWS, ff), BF), v((n_rows, d), BF),
+            v((2, R, LANES), F32), v((2, R, seq), F32), v((2, R, seq), F32), v((2, R, LANES), F32),
+            *[v((n_rows // 2, d), F32)] * 6,
             dma((12,)), dma((3,)), dma((SLOTS,)), dma((SLOTS,)), dma((n_sub,)), dma((n_remote,)), dma((n_remote,)),
         ]
         return pl.pallas_call(

time: 70.2 us -> 61.5 us (0.88)
  Pallas kernels: 68.2 us -> 59.5 us
    pallas_call x1, Pallas kernels: 68.2 us -> 59.5 us  [device_step(): pl.pallas_call(functools.partial(layer_kernel, cfg), out_shape=jax.ShapeD...]
where the time goes in v3:
time: 61.5 us; the launch traced here: 61.4 us
  Pallas kernels  59.5 us (97%)
  local copies, waits for them, and re-layouts  1.87 us (3%)
    pallas_call x1, Pallas kernels, device_step(): pl.pallas_call(functools.partial(layer_kernel, cfg), out_shape=jax.ShapeD...  59.5 us
    unnamed x1, local copies, waits for them, and re-layouts  1.87 us

profile of v3, /device:TPU:0, one launch (start us, length us, event | category | flops | bytes accessed | tf_op | source)
XLA Modules:
  0.0 61.4 jit_solution(289600385420337523)
XLA Ops:
  0.0 59.5 %layer.1 = bf16[256,1024]{1,0:T(8,128)(2,1)} custom-call(bf16[256,1024]{1,0:T(8,128)(2,1)} %hid_hbm.1, f32[1,1024]{1,0:T(1,128)} %bitcast.13, bf16[1024,512]{1,0:T(8,128)(2,1)} %wq_hbm.1, bf16[1024,256]{1,0:T(8,128)(2,1)} %wk_hbm.1, bf16[1024,256]{1,0:T(8,128)(2,1)} %wv_hbm.1, bf16[512,1024]{1,0:T(8,128)(2,1)} %wo_hbm.1, bf16[256,256,256]{2,1,0:T(8,128)(2,1)} %bitcast.9, ...), custom_call_target="tpu_custom_call" | custom-call | tf_op jit(solution)/shard_map/layer/pallas_call | solution.py:445
  59.5 1.9 %copy.19 = bf16[256,1024]{1,0:T(8,128)(2,1)} copy(bf16[256,1024]{1,0:T(8,128)(2,1)} %layer.1) | data formatting | bytes 1048576

commit v4 on v3

--- a/solution.py
+++ b/solution.py
@@ -35,7 +35,7 @@
 def layer_kernel(cfg, hid_hbm, gn_hbm, wq_hbm, wk_hbm, wv_hbm, wo_hbm, k_hbm, v_hbm, len_hbm, wsg_hbm, wsu_hbm, wsd_hbm,
                  wg_hbm, wu_hbm, wd_hbm, ids_hbm, gts_hbm, out_hbm,
                  hall, xall, gn, wq, wk, wv, wo, wsg, wsu, wsd, wg, wu, wd, idg, gtg, gb, kbuf, vbuf, lens,
-                 q0, q1, kn, vn, om, dense, part, rpf, rph, act, outb, ss, sc, ps, sp, tf, ryf, xs, rxf, ty, ryo,
+                 q0, q1, kn, vn, om, dense, part, rpf, rph, act, outb, ss, sc, ps, sp, tf, ryf, xs, rxf, ty, ryo, xa, rxa, ryl,
                  lsem, wsem, ksem, vsem, osem, s_send, s_recv):
     n_rows, kvh, hd, seq, n_local, tp_size, ep_size = cfg
     d_model = hall.shape[2]
@@ -79,7 +79,8 @@
                 local(gn_hbm, gn, lsem.at[3]), local(len_hbm, lens, lsem.at[4])]
     qkv_cp = [local(wq_hbm, wq, lsem.at[5]), local(wk_hbm, wk, lsem.at[6]), local(wv_hbm, wv, lsem.at[7])]
     sh_cp = [local(wsg_hbm, wsg, lsem.at[8]), local(wsu_hbm, wsu, lsem.at[9]), local(wsd_hbm, wsd, lsem.at[10]),
-             local(wo_hbm, wo, lsem.at[11])]
+             *[local(wo_hbm.at[pl.ds((h * 2 + g) * hd, hd)], wo.at[pl.ds((g * kvh + h) * hd, hd)], osem.at[len(SUBS) + g * kvh + h])
+               for g in range(2) for h in range(kvh)]]
     exp_cp = [local(wg_hbm, wg, wsem.at[0]), local(wu_hbm, wu, wsem.at[1]), local(wd_hbm, wd, wsem.at[2])]
 
     def k_cp(b):
@@ -108,8 +109,15 @@
         pl.semaphore_signal(barrier, inc=1, device_id=dev, device_id_type=pl.DeviceIdType.MESH)
     pl.semaphore_wait(barrier, 3)
 
+    def whole(s):
+        return pl.ds(*SUBS[s])
+
     chunks = range(n_chunk)
     subs = range(len(SUBS))
+
+    def sub_of(i):
+        return [s for s in subs if SUBS[s][0] // ROWS == i]
+
     x_hid = [remote(hall.at[0, rows(i)], hall.at[2, rows(i)], xnbr) for i in chunks]
     p_hid = [remote(hall.at[0, rows(i)], hall.at[1, rows(i)], partner) for i in chunks]
     f_hid = [remote(hall.at[2, rows(i)], hall.at[3, rows(i)], partner) for i in chunks]
@@ -118,10 +126,17 @@
     f_idg = [remote(idg.at[2], idg.at[3], partner), remote(gtg.at[2], gtg.at[3], partner)]
     c_far = [remote(part.at[3, rows(i)], rpf.at[rows(i)], partner) for i in chunks]
     c_near = [remote(part.at[1, rows(i)], rph.at[rows(i)], partner) for i in chunks]
-    y_far = [remote(tf.at[packed(s)], ryf.at[packed(s)], ynbr) for s in subs]
-    x_ret = [remote(xs.at[packed(s)], rxf.at[packed(s)], xnbr) for s in subs]
-    y_own = [remote(ty.at[packed(s)], ryo.at[packed(s)], ynbr) for s in subs]
-    y_out = [remote(outb.at[mine(s)], outb.at[mine(s)], ynbr) for s in subs]
+    def packed2(s):
+        return pl.ds(first.index(s) * SUBS[s][1], SUBS[s][1])
+
+    first, last = [2], subs[-1]
+    far_subs = [s for s in subs if s not in first]
+    x_all = {s: remote(xa.at[packed2(s)], rxa.at[packed2(s)], xnbr) for s in first}
+    y_last = remote(dense.at[whole(last)], ryl, ynbr)
+    y_far = {s: remote(tf.at[packed(s)], ryf.at[packed(s)], ynbr) for s in far_subs}
+    x_ret = {s: remote(xs.at[packed(s)], rxf.at[packed(s)], xnbr) for s in far_subs}
+    y_own = [remote(ty.at[packed(s)], ryo.at[packed(s)], ynbr) for s in subs[:-1]]
+    y_out = [remote(outb.at[mine(s)], outb.at[mine(s)], ynbr) for s in subs[:-1]]
 
     for c in small_cp:
         c.wait()
@@ -134,12 +149,13 @@
 
     def normalize(grp, r0, n):
         def body(j, carry):
-            at = pl.ds(pl.multiple_of(r0 + j * 32, 32), 32)
-            h32 = hall[grp, at, :].astype(F32)
-            inv = lax.rsqrt(jnp.mean(h32 * h32, axis=-1, keepdims=True) + RMS_EPS)
-            xall[grp, at, :] = (h32 * inv * gn[...]).astype(BF)
+            for k in range(4):
+                at = pl.ds(pl.multiple_of(r0 + j * 128 + k * 32, 32), 32)
+                h32 = hall[grp, at, :].astype(F32)
+                inv = lax.rsqrt(jnp.mean(h32 * h32, axis=-1, keepdims=True) + RMS_EPS)
+                xall[grp, at, :] = (h32 * inv * gn[...]).astype(BF)
             return carry
-        lax.fori_loop(0, n // 32, body, 0)
+        lax.fori_loop(0, n // 128, body, 0)
 
     first_exp = (ep * tp_size + tp) * n_local
 
@@ -264,18 +280,20 @@
                     for k in range(j * n_down // n_up, (j + 1) * n_down // n_up):
                         down(e - 1, k)
 
-    def sub_of(i):
-        return [s for s in subs if SUBS[s][0] // ROWS == i]
-
-    def far_y(i):
+    def far_send(i):
         c_far[i].wait_recv()
-        for s in sub_of(i):
-            at = theirs(s)
-            tf[packed(s), :] = part[2, at, :] + rpf[at, :]
-            y_far[s].start()
-
-    def far_x(i):
-        for s in sub_of(i):
+        for s in sub_of(i)[::-1]:
+            if s in first:
+                at = whole(s)
+                xa[packed2(s), :] = part[2, at, :] + rpf[at, :]
+                x_all[s].start()
+            else:
+                at = theirs(s)
+                tf[packed(s), :] = part[2, at, :] + rpf[at, :]
+                y_far[s].start()
+
+    def far_x(some):
+        for s in some:
             y_far[s].wait_recv()
             at = mine(s)
             xs[packed(s), :] = part[2, at, :] + rpf[at, :] + ryf[packed(s), :]
@@ -308,8 +326,6 @@
             cs = slice(j * 256, (j + 1) * 256)
             dense[:, cs] = dotf(sa, wsd[:, cs])
 
-    swap = one_hot_mat(2 * kd, 2 * kd, lambda r, c: ((r // kd) == ((c // hd) % 2)) & ((r % kd) // hd == c // (2 * hd)) & (r % hd == c % hd))
-
     def own_y(s):
         r0, n = SUBS[s]
         if s in (sub_of(0)[0], sub_of(1)[0]):
@@ -317,18 +333,34 @@
         at = pl.ds(r0, n)
         gather_o = one_hot_mat(2 * n, n * per_tok, lambda r, c: (c // per_tok == r % n) & ((c % per_tok) // kvh == r // n))
         o2 = dotf(gather_o, om[pl.ds(r0 * per_tok, n * per_tok), :].astype(BF)).astype(BF)
-        ctx_bf = dotf(jnp.concatenate([o2[0:n], o2[n:2 * n]], axis=1), swap).astype(BF)
+        ctx_bf = jnp.concatenate([o2[0:n], o2[n:2 * n]], axis=1)
+        if s in first:
+            x_all[s].wait_recv()
         for j in range(d_model // 256):
             cs = slice(j * 256, (j + 1) * 256)
-            dense[at, cs] = dense[at, cs] + dotf(ctx_bf, wo[:, cs]) + part[0, at, cs] + rph[at, cs]
-        ty[packed(s), :] = dense[theirs(s), :]
-        y_own[s].start()
+            total = dense[at, cs] + dotf(ctx_bf, wo[:, cs]) + part[0, at, cs] + rph[at, cs]
+            dense[at, cs] = total + rxa[packed2(s), cs] if s in first else total
+        if s == last:
+            x_ret[s].wait_recv()
+            dense[mine(s), :] = dense[mine(s), :] + rxf[packed(s), :]
+            y_last.start()
+        else:
+            ty[packed(s), :] = dense[theirs(s), :]
+            y_own[s].start()
 
     def finish(s):
+        if s == last:
+            at = whole(s)
+            y_last.wait_recv()
+            outb[at, :] = (hall[0, at, :].astype(F32) + (dense[at, :] + ryl[...])).astype(BF)
+            return
+        at = mine(s)
         y_own[s].wait_recv()
-        x_ret[s].wait_recv()
-        at = mine(s)
-        outb[at, :] = (hall[0, at, :].astype(F32) + (dense[at, :] + ryo[packed(s), :] + rxf[packed(s), :])).astype(BF)
+        total = dense[at, :] + ryo[packed(s), :]
+        if s in far_subs:
+            x_ret[s].wait_recv()
+            total = total + rxf[packed(s), :]
+        outb[at, :] = (hall[0, at, :].astype(F32) + total).astype(BF)
         y_out[s].start()
 
     normalize(0, 0, n_rows)
@@ -349,7 +381,7 @@
     kn[...] = dotf(xall[0], wk[...]).astype(BF).astype(F32)
     vn[...] = dotf(xall[0], wv[...]).astype(BF).astype(F32)
 
-    attend(8)
+    attend(6)
     for c in p_idg + x_idg:
         c.wait_recv()
     for c in f_idg:
@@ -357,48 +389,49 @@
     gate_table(0)
     gate_table(1)
     gate_table(2)
-    attend(10)
-    arrive(0)
     for c in exp_cp:
         c.wait()
-    attend(12)
+    near(0)
+    arrive(0)
+    attend(8)
     for c in f_idg:
         c.wait_recv()
     gate_table(3)
     far(0)
     arrive(1)
+    attend(12)
+    far_send(0)
+    far(1)
+    shared_expert()
+    own_y(0)
     attend(14)
-    far_y(0)
-    far(1)
+    far_send(1)
+    near(1)
+    far_x([0, 1])
     attend(18)
-    far_y(1)
-    near(0)
-    shared_expert()
-    far_x(0)
-    near(1)
-    own_y(0)
     own_y(1)
     attend(22)
-    far_x(1)
+    far_x([4, 3])
     attend(26)
+    finish(0)
     own_y(2)
-    finish(0)
-    finish(1)
     attend(30)
     own_y(3)
-    finish(2)
+    finish(1)
     attend(n_blk)
     own_y(4)
+    finish(2)
     finish(3)
     finish(4)
     out_cp = []
     for s in subs:
-        y_out[s].wait_recv()
-        at = pl.ds(*SUBS[s])
+        if s != last:
+            y_out[s].wait_recv()
+        at = whole(s)
         c = local(outb.at[at], out_hbm.at[at], osem.at[s])
         c.start()
         out_cp.append(c)
-    for c in x_hid + p_hid + f_hid + x_idg + p_idg + f_idg + c_far + c_near + y_far + x_ret + y_own + y_out:
+    for c in x_hid + p_hid + f_hid + x_idg + p_idg + f_idg + c_far + c_near + list(x_all.values()) + list(y_far.values()) + list(x_ret.values()) + y_own + y_out + [y_last]:
         c.wait_send()
     for c in out_cp:
         c.wait()
@@ -439,8 +472,8 @@
             v((n_rows, kd), F32), v((n_rows, kd), F32), v((n_rows, kd), F32), v((n_rows, kd), F32), v((n_rows * 2 * kvh, kd), F32),
             v((n_rows, d), F32), v((4, n_rows, d), F32), v((n_rows, d), F32), v((n_rows, d), F32), v((2, 2 * ROWS, ff), BF), v((n_rows, d), BF),
             v((2, R, LANES), F32), v((2, R, seq), F32), v((2, R, seq), F32), v((2, R, LANES), F32),
-            *[v((n_rows // 2, d), F32)] * 6,
-            dma((12,)), dma((3,)), dma((SLOTS,)), dma((SLOTS,)), dma((n_sub,)), dma((n_remote,)), dma((n_remote,)),
+            *[v((n_rows // 2, d), F32)] * 6, v((ROWS, d), F32), v((ROWS, d), F32), v((SUBS[-1][1], d), F32),
+            dma((12,)), dma((3,)), dma((SLOTS,)), dma((SLOTS,)), dma((n_sub + 2 * kvh,)), dma((n_remote,)), dma((n_remote,)),
         ]
         return pl.pallas_call(
             functools.partial(layer_kernel, cfg),

time: 61.5 us -> 58.4 us (0.950)
  Pallas kernels: 59.5 us -> 56.4 us
    pallas_call x1, Pallas kernels: 59.5 us -> 56.4 us  [device_step(): pl.pallas_call(functools.partial(layer_kernel, cfg), out_shape=jax.ShapeD...]
where the time goes in v4:
time: 58.4 us; the launch traced here: 58.3 us
  Pallas kernels  56.4 us (97%)
  local copies, waits for them, and re-layouts  1.87 us (3%)
    pallas_call x1, Pallas kernels, device_step(): pl.pallas_call(functools.partial(layer_kernel, cfg), out_shape=jax.ShapeD...  56.4 us
    unnamed x1, local copies, waits for them, and re-layouts  1.87 us

profile of v4, /device:TPU:0, one launch (start us, length us, event | category | flops | bytes accessed | tf_op | source)
XLA Modules:
  0.0 58.3 jit_solution(16869797530728724393)
XLA Ops:
  0.0 56.4 %layer.1 = bf16[256,1024]{1,0:T(8,128)(2,1)} custom-call(bf16[256,1024]{1,0:T(8,128)(2,1)} %hid_hbm.1, f32[1,1024]{1,0:T(1,128)} %bitcast.13, bf16[1024,512]{1,0:T(8,128)(2,1)} %wq_hbm.1, bf16[1024,256]{1,0:T(8,128)(2,1)} %wk_hbm.1, bf16[1024,256]{1,0:T(8,128)(2,1)} %wv_hbm.1, bf16[512,1024]{1,0:T(8,128)(2,1)} %wo_hbm.1, bf16[256,256,256]{2,1,0:T(8,128)(2,1)} %bitcast.9, ...), custom_call_target="tpu_custom_call" | custom-call | tf_op jit(solution)/shard_map/layer/pallas_call | solution.py:478
  56.4 1.9 %copy.19 = bf16[256,1024]{1,0:T(8,128)(2,1)} copy(bf16[256,1024]{1,0:T(8,128)(2,1)} %layer.1) | data formatting | bytes 1048576
